TPU v7x, 512 devices: a whole 4x8x8 slice. The times are simulated.
512 devices in a mesh: dp: 64 (over x, y, core), rank: 8 (over z).
Axes of the slice: x: 4, y: 8, z: 8, core: 2. Of those that a mesh axis runs over, the one named last changes fastest.
Arguments:
- cloud_x: float32 [64, 131072], P(None, 'dp'), may hold values from -0.6 to 0.6
- cloud_y: float32 [64, 131072], P(None, 'dp'), may hold values from -0.6 to 0.6
- mass_x: float32 [131072], P('dp'), may hold values from 0.25 to 4
- mass_y: float32 [131072], P('dp'), may hold values from 0.25 to 4
- left_start: float32 [256, 131072], P('rank', 'dp'), may hold values from 0.25 to 204.8
- right_start: float32 [256, 131072], P('rank', 'dp'), may hold values from 0.25 to 204.8
- weight_start: float32 [256], P('rank'), may hold values from 0.25 to 4
Outputs:
- left_factor: float32 [256, 131072], P('rank', 'dp')
- right_factor: float32 [256, 131072], P('rank', 'dp')
- rank_weights: float32 [256], P('rank')
All inputs are finite; a program needn't handle non-finite values.
Results may differ from a plain program's by a relative error of at most 0.0003.
Values sent between devices are 32-bit elements; how exact they have to be, the bound alone decides.
A program may use at most 64 MiB of HBM per device.

v0:
```python
import jax
import jax.numpy as jnp
from jax import lax
from jax.sharding import PartitionSpec as P

RANK = 256
INNER = 4
MIRROR = 3


exact_mode = lax.Precision.HIGHEST
step_size = 2.0


def from_everyone(value, axis):
    length = lax.axis_size(axis)
    return lax.all_to_all(
        jnp.broadcast_to(value[None], (length, *value.shape)), axis, 0, 0, tiled=True
    )


def of_everyone(value, axis):
    return from_everyone(value, axis).sum(axis=0)


def in_one(arrays, axis):
    ends = [0]
    for a in arrays:
        ends.append(ends[-1] + a.size)
    total = of_everyone(jnp.concatenate([a.ravel() for a in arrays]), axis)
    return tuple((total[b:e].reshape(a.shape) for a, b, e in zip(arrays, ends, ends[1:])))


def moments(cloud, factor):
    product = jnp.dot(cloud, factor.T, precision=exact_mode)
    square = jnp.dot(factor, jnp.sum(cloud * cloud, axis=0), precision=exact_mode)
    column = jnp.sum(factor, axis=1)
    return (product, square, column)


def shards(cloud_x, cloud_y, mass_x, mass_y, left_start, right_start, weight_start):
    ranks_local = left_start.shape[0]
    points_dev = left_start.shape[1]
    total_count = float(points_dev * lax.axis_size("dp"))
    mass_sums = in_one((jnp.sum(mass_x), jnp.sum(mass_y)), "dp")
    left_mass = mass_x * (total_count / mass_sums[0])
    right_mass = mass_y * (total_count / mass_sums[1])

    def project(kernel_left, kernel_right, kernel_weight):
        scale_left = jnp.ones((ranks_local,), jnp.float32)
        scale_right = jnp.ones((ranks_local,), jnp.float32)
        for repeat in range(INNER):
            row_left, row_right = in_one(
                (
                    jnp.dot(scale_left, kernel_left, precision=exact_mode),
                    jnp.dot(scale_right, kernel_right, precision=exact_mode),
                ),
                "rank",
            )
            point_left = left_mass / row_left
            point_right = right_mass / row_right
            column_left, column_right = in_one(
                (
                    jnp.dot(kernel_left, point_left, precision=exact_mode),
                    jnp.dot(kernel_right, point_right, precision=exact_mode),
                ),
                "dp",
            )
            weights = jnp.cbrt(
                kernel_weight * scale_left * column_left * scale_right * column_right
            )
            scale_left = weights / column_left
            scale_right = weights / column_right
        left = point_left[None, :] * kernel_left * scale_left[:, None]
        right = point_right[None, :] * kernel_right * scale_right[:, None]
        return (left, right, weights)

    left, right, weights = project(left_start, right_start, weight_start)
    for outer in range(MIRROR):
        prod_x, square_x, sums_q = moments(cloud_x, left)
        prod_y, square_y, sums_r = moments(cloud_y, right)
        prod_x, prod_y, square_x, square_y, sums_q, sums_r = in_one(
            (prod_x, prod_y, square_x, square_y, sums_q, sums_r), "dp"
        )
        grad_q = square_y / weights
        grad_r = square_x / weights
        grad_g = -(
            square_x * sums_r + sums_q * square_y - 2.0 * jnp.sum(prod_x * prod_y, axis=0)
        ) / (weights * weights)
        total_q, total_r, total_g = in_one(
            (jnp.sum(grad_q), jnp.sum(grad_r), jnp.sum(grad_g)), "rank"
        )
        mean_q = total_q / RANK
        mean_r = total_r / RANK
        mean_g = total_g / RANK
        field_q = (grad_q - mean_q)[:, None] - 2.0 * jnp.dot(
            prod_y.T, cloud_x, precision=exact_mode
        ) / weights[:, None]
        field_r = (grad_r - mean_r)[:, None] - 2.0 * jnp.dot(
            prod_x.T, cloud_y, precision=exact_mode
        ) / weights[:, None]
        kernel_left = left * jnp.exp(-step_size * field_q)
        kernel_right = right * jnp.exp(-step_size * field_r)
        kernel_weight = weights * jnp.exp(-step_size * (grad_g - mean_g))
        left, right, weights = project(kernel_left, kernel_right, kernel_weight)
    return (RANK * left, RANK * right, weights * (RANK / total_count))


def solution(mesh):
    in_specs = (
        P(None, "dp"),
        P(None, "dp"),
        P("dp"),
        P("dp"),
        P("rank", "dp"),
        P("rank", "dp"),
        P("rank"),
    )
    out_specs = (P("rank", "dp"), P("rank", "dp"), P("rank"))
    return jax.shard_map(shards, mesh=mesh, in_specs=in_specs, out_specs=out_specs, check_vma=False)
```

profile of v0, /device:TPU:1, one launch (start us, length us, event | category | flops | bytes accessed | tf_op | source)
XLA Modules:
  0.0 634.7 jit_solution(5583959564733694816)
XLA Ops:
  5.3 11.6 %all-to-all-start = ((f32[64,1,2]{2,1,0:T(1,128)}), f32[64,1,2]{2,1,0:T(1,128)S(1)}, u32[]{:S(2)}, u32[]{:S(2)}) async-start(f32[64,1,2]{2,1,0:T(1,128)} %broadcast_in_dim.78), calls=%async_computation | async-start | bytes 65536 | tf_op jit(solution)/shard_map/all_to_all | solution.py:17
  19.4 6.8 %all-to-all-done = f32[64,1,2]{2,1,0:T(1,128)S(1)} async-done(((f32[64,1,2]{2,1,0:T(1,128)}), f32[64,1,2]{2,1,0:T(1,128)S(1)}, u32[]{:S(2)}, u32[]{:S(2)}) %all-to-all-start) | async-done | bytes 544 | tf_op jit(solution)/shard_map/all_to_all | solution.py:17
  26.9 10.0 %all-to-all-start.1 = ((f32[8,1,4096]{2,1,0:T(1,128)}), f32[8,1,4096]{2,1,0:T(1,128)S(1)}, u32[]{:S(2)}, u32[]{:S(2)}) async-start(f32[8,1,4096]{2,1,0:T(1,128)} %broadcast_in_dim.79), calls=%async_computation.1 | async-start | bytes 262144 | tf_op jit(solution)/shard_map/all_to_all | solution.py:17
  39.0 5.7 all-to-all-done.1
  45.6 15.0 %all_to_all.234 = f32[64,1,64]{2,1,0:T(1,128)S(1)} all-to-all(f32[64,1,64]{2,1,0:T(1,128)S(1)} %broadcast_in_dim.80), channel_id=1, replica_groups=mesh['dp'=64,'rank'=8] {'dp'}, dimensions={0} | all-to-all | bytes 32768 | tf_op jit(solution)/shard_map/all_to_all | solution.py:17
  61.4 10.2 %all_to_all.235 = f32[8,1,4096]{2,1,0:T(1,128)S(1)} all-to-all(f32[8,1,4096]{2,1,0:T(1,128)S(1)} %broadcast_in_dim.81), channel_id=1, replica_groups=mesh['dp'=64,'rank'=8] {'rank'}, dimensions={0} | all-to-all | bytes 262144 | tf_op jit(solution)/shard_map/all_to_all | solution.py:17
  72.5 14.8 %all_to_all.236 = f32[64,1,64]{2,1,0:T(1,128)S(1)} all-to-all(f32[64,1,64]{2,1,0:T(1,128)S(1)} %broadcast_in_dim.82), channel_id=1, replica_groups=mesh['dp'=64,'rank'=8] {'dp'}, dimensions={0} | all-to-all | bytes 32768 | tf_op jit(solution)/shard_map/all_to_all | solution.py:17
  88.1 10.4 %all_to_all.237 = f32[8,1,4096]{2,1,0:T(1,128)S(1)} all-to-all(f32[8,1,4096]{2,1,0:T(1,128)S(1)} %broadcast_in_dim.83), channel_id=1, replica_groups=mesh['dp'=64,'rank'=8] {'rank'}, dimensions={0} | all-to-all | bytes 262144 | tf_op jit(solution)/shard_map/all_to_all | solution.py:17
  99.3 14.8 %all_to_all.238 = f32[64,1,64]{2,1,0:T(1,128)S(1)} all-to-all(f32[64,1,64]{2,1,0:T(1,128)S(1)} %broadcast_in_dim.84), channel_id=1, replica_groups=mesh['dp'=64,'rank'=8] {'dp'}, dimensions={0} | all-to-all | bytes 32768 | tf_op jit(solution)/shard_map/all_to_all | solution.py:17
  115.6 3.4 all-to-all-start.7
  119.0 7.7 %all-to-all-done.7 = f32[8,1,4096]{2,1,0:T(1,128)S(1)} async-done(((f32[8,1,4096]{2,1,0:T(1,128)}), f32[8,1,4096]{2,1,0:T(1,128)S(1)}, u32[]{:S(2)}, u32[]{:S(2)}) %all-to-all-start.7) | async-done | bytes 131104 | tf_op jit(solution)/shard_map/all_to_all | solution.py:17
  128.2 6.2 all-to-all-start.8
  134.5 9.3 %all-to-all-done.8 = f32[64,1,64]{2,1,0:T(1,128)S(1)} async-done(((f32[64,1,64]{2,1,0:T(1,128)}), f32[64,1,64]{2,1,0:T(1,128)S(1)}, u32[]{:S(2)}, u32[]{:S(2)}) %all-to-all-start.8) | async-done | bytes 16416 | tf_op jit(solution)/shard_map/all_to_all | solution.py:17
  147.1 33.6 %all_to_all.239 = f32[64,1,4224]{2,1,0:T(1,128)S(1)} all-to-all(f32[64,1,4224]{2,1,0:T(1,128)S(1)} %broadcast_in_dim.87), channel_id=1, replica_groups=mesh['dp'=64,'rank'=8] {'dp'}, dimensions={0} | all-to-all | bytes 2162688 | tf_op jit(solution)/shard_map/all_to_all | solution.py:17
  182.3 2.0 pad_maximum_fusion.21
  184.3 8.9 %all_to_all.240 = f32[8,1,3]{2,1,0:T(1,128)S(1)} all-to-all(f32[8,1,3]{2,1,0:T(1,128)S(1)} %broadcast_in_dim.88), channel_id=1, replica_groups=mesh['dp'=64,'rank'=8] {'rank'}, dimensions={0} | all-to-all | bytes 192 | tf_op jit(solution)/shard_map/all_to_all | solution.py:17
  196.7 10.4 %all_to_all.241 = f32[8,1,4096]{2,1,0:T(1,128)S(1)} all-to-all(f32[8,1,4096]{2,1,0:T(1,128)S(1)} %broadcast_in_dim.89), channel_id=1, replica_groups=mesh['dp'=64,'rank'=8] {'rank'}, dimensions={0} | all-to-all | bytes 262144 | tf_op jit(solution)/shard_map/all_to_all | solution.py:17
  208.6 8.5 %all-to-all-start.12 = ((f32[64,1,64]{2,1,0:T(1,128)}), f32[64,1,64]{2,1,0:T(1,128)S(1)}, u32[]{:S(2)}, u32[]{:S(2)}) async-start(f32[64,1,64]{2,1,0:T(1,128)} %broadcast_in_dim.90), calls=%async_computation.12 | async-start | bytes 65536 | tf_op jit(solution)/shard_map/all_to_all | solution.py:17
  217.8 8.6 %all-to-all-done.12 = f32[64,1,64]{2,1,0:T(1,128)S(1)} async-done(((f32[64,1,64]{2,1,0:T(1,128)}), f32[64,1,64]{2,1,0:T(1,128)S(1)}, u32[]{:S(2)}, u32[]{:S(2)}) %all-to-all-start.12) | async-done | bytes 16416 | tf_op jit(solution)/shard_map/all_to_all | solution.py:17
  227.1 10.2 %all_to_all.242 = f32[8,1,4096]{2,1,0:T(1,128)S(1)} all-to-all(f32[8,1,4096]{2,1,0:T(1,128)S(1)} %broadcast_in_dim.91), channel_id=1, replica_groups=mesh['dp'=64,'rank'=8] {'rank'}, dimensions={0} | all-to-all | bytes 262144 | tf_op jit(solution)/shard_map/all_to_all | solution.py:17
  238.2 14.8 %all_to_all.243 = f32[64,1,64]{2,1,0:T(1,128)S(1)} all-to-all(f32[64,1,64]{2,1,0:T(1,128)S(1)} %broadcast_in_dim.92), channel_id=1, replica_groups=mesh['dp'=64,'rank'=8] {'dp'}, dimensions={0} | all-to-all | bytes 32768 | tf_op jit(solution)/shard_map/all_to_all | solution.py:17
  253.8 10.2 %all_to_all.244 = f32[8,1,4096]{2,1,0:T(1,128)S(1)} all-to-all(f32[8,1,4096]{2,1,0:T(1,128)S(1)} %broadcast_in_dim.93), channel_id=1, replica_groups=mesh['dp'=64,'rank'=8] {'rank'}, dimensions={0} | all-to-all | bytes 262144 | tf_op jit(solution)/shard_map/all_to_all | solution.py:17
  264.9 14.8 %all_to_all.245 = f32[64,1,64]{2,1,0:T(1,128)S(1)} all-to-all(f32[64,1,64]{2,1,0:T(1,128)S(1)} %broadcast_in_dim.94), channel_id=1, replica_groups=mesh['dp'=64,'rank'=8] {'dp'}, dimensions={0} | all-to-all | bytes 32768 | tf_op jit(solution)/shard_map/all_to_all | solution.py:17
  280.5 10.2 %all_to_all.246 = f32[8,1,4096]{2,1,0:T(1,128)S(1)} all-to-all(f32[8,1,4096]{2,1,0:T(1,128)S(1)} %broadcast_in_dim.95), channel_id=1, replica_groups=mesh['dp'=64,'rank'=8] {'rank'}, dimensions={0} | all-to-all | bytes 262144 | tf_op jit(solution)/shard_map/all_to_all | solution.py:17
  291.6 15.1 %all_to_all.247 = f32[64,1,64]{2,1,0:T(1,128)S(1)} all-to-all(f32[64,1,64]{2,1,0:T(1,128)S(1)} %broadcast_in_dim.96), channel_id=1, replica_groups=mesh['dp'=64,'rank'=8] {'dp'}, dimensions={0} | all-to-all | bytes 32768 | tf_op jit(solution)/shard_map/all_to_all | solution.py:17
  310.2 33.2 %all_to_all.248 = f32[64,1,4224]{2,1,0:T(1,128)S(1)} all-to-all(f32[64,1,4224]{2,1,0:T(1,128)S(1)} %broadcast_in_dim.97), channel_id=1, replica_groups=mesh['dp'=64,'rank'=8] {'dp'}, dimensions={0} | all-to-all | bytes 2162688 | tf_op jit(solution)/shard_map/all_to_all | solution.py:17
  344.9 2.0 pad_maximum_fusion.26
  346.9 8.9 %all_to_all.249 = f32[8,1,3]{2,1,0:T(1,128)S(1)} all-to-all(f32[8,1,3]{2,1,0:T(1,128)S(1)} %broadcast_in_dim.98), channel_id=1, replica_groups=mesh['dp'=64,'rank'=8] {'rank'}, dimensions={0} | all-to-all | bytes 192 | tf_op jit(solution)/shard_map/all_to_all | solution.py:17
  359.3 10.4 %all_to_all.250 = f32[8,1,4096]{2,1,0:T(1,128)S(1)} all-to-all(f32[8,1,4096]{2,1,0:T(1,128)S(1)} %broadcast_in_dim.99), channel_id=1, replica_groups=mesh['dp'=64,'rank'=8] {'rank'}, dimensions={0} | all-to-all | bytes 262144 | tf_op jit(solution)/shard_map/all_to_all | solution.py:17
  371.2 8.5 %all-to-all-start.22 = ((f32[64,1,64]{2,1,0:T(1,128)}), f32[64,1,64]{2,1,0:T(1,128)S(1)}, u32[]{:S(2)}, u32[]{:S(2)}) async-start(f32[64,1,64]{2,1,0:T(1,128)} %broadcast_in_dim.100), calls=%async_computation.22 | async-start | bytes 65536 | tf_op jit(solution)/shard_map/all_to_all | solution.py:17
  380.4 8.6 %all-to-all-done.22 = f32[64,1,64]{2,1,0:T(1,128)S(1)} async-done(((f32[64,1,64]{2,1,0:T(1,128)}), f32[64,1,64]{2,1,0:T(1,128)S(1)}, u32[]{:S(2)}, u32[]{:S(2)}) %all-to-all-start.22) | async-done | bytes 16416 | tf_op jit(solution)/shard_map/all_to_all | solution.py:17
  389.7 10.2 %all_to_all.251 = f32[8,1,4096]{2,1,0:T(1,128)S(1)} all-to-all(f32[8,1,4096]{2,1,0:T(1,128)S(1)} %broadcast_in_dim.101), channel_id=1, replica_groups=mesh['dp'=64,'rank'=8] {'rank'}, dimensions={0} | all-to-all | bytes 262144 | tf_op jit(solution)/shard_map/all_to_all | solution.py:17
  400.8 14.8 %all_to_all.252 = f32[64,1,64]{2,1,0:T(1,128)S(1)} all-to-all(f32[64,1,64]{2,1,0:T(1,128)S(1)} %broadcast_in_dim.102), channel_id=1, replica_groups=mesh['dp'=64,'rank'=8] {'dp'}, dimensions={0} | all-to-all | bytes 32768 | tf_op jit(solution)/shard_map/all_to_all | solution.py:17
  416.4 10.2 %all_to_all.253 = f32[8,1,4096]{2,1,0:T(1,128)S(1)} all-to-all(f32[8,1,4096]{2,1,0:T(1,128)S(1)} %broadcast_in_dim.103), channel_id=1, replica_groups=mesh['dp'=64,'rank'=8] {'rank'}, dimensions={0} | all-to-all | bytes 262144 | tf_op jit(solution)/shard_map/all_to_all | solution.py:17
  427.6 14.8 %all_to_all.254 = f32[64,1,64]{2,1,0:T(1,128)S(1)} all-to-all(f32[64,1,64]{2,1,0:T(1,128)S(1)} %broadcast_in_dim.104), channel_id=1, replica_groups=mesh['dp'=64,'rank'=8] {'dp'}, dimensions={0} | all-to-all | bytes 32768 | tf_op jit(solution)/shard_map/all_to_all | solution.py:17
  443.2 10.4 %all_to_all.255 = f32[8,1,4096]{2,1,0:T(1,128)S(1)} all-to-all(f32[8,1,4096]{2,1,0:T(1,128)S(1)} %broadcast_in_dim.105), channel_id=1, replica_groups=mesh['dp'=64,'rank'=8] {'rank'}, dimensions={0} | all-to-all | bytes 262144 | tf_op jit(solution)/shard_map/all_to_all | solution.py:17
  454.5 14.8 %all_to_all.256 = f32[64,1,64]{2,1,0:T(1,128)S(1)} all-to-all(f32[64,1,64]{2,1,0:T(1,128)S(1)} %broadcast_in_dim.106), channel_id=1, replica_groups=mesh['dp'=64,'rank'=8] {'dp'}, dimensions={0} | all-to-all | bytes 32768 | tf_op jit(solution)/shard_map/all_to_all | solution.py:17
  472.8 33.2 %all_to_all.257 = f32[64,1,4224]{2,1,0:T(1,128)S(1)} all-to-all(f32[64,1,4224]{2,1,0:T(1,128)S(1)} %broadcast_in_dim.107), channel_id=1, replica_groups=mesh['dp'=64,'rank'=8] {'dp'}, dimensions={0} | all-to-all | bytes 2162688 | tf_op jit(solution)/shard_map/all_to_all | solution.py:17
  509.5 8.9 %all_to_all.258 = f32[8,1,3]{2,1,0:T(1,128)S(1)} all-to-all(f32[8,1,3]{2,1,0:T(1,128)S(1)} %broadcast_in_dim.108), channel_id=1, replica_groups=mesh['dp'=64,'rank'=8] {'rank'}, dimensions={0} | all-to-all | bytes 192 | tf_op jit(solution)/shard_map/all_to_all | solution.py:17
  521.9 10.4 %all_to_all.259 = f32[8,1,4096]{2,1,0:T(1,128)S(1)} all-to-all(f32[8,1,4096]{2,1,0:T(1,128)S(1)} %broadcast_in_dim.109), channel_id=1, replica_groups=mesh['dp'=64,'rank'=8] {'rank'}, dimensions={0} | all-to-all | bytes 262144 | tf_op jit(solution)/shard_map/all_to_all | solution.py:17
  533.8 8.5 %all-to-all-start.32 = ((f32[64,1,64]{2,1,0:T(1,128)}), f32[64,1,64]{2,1,0:T(1,128)S(1)}, u32[]{:S(2)}, u32[]{:S(2)}) async-start(f32[64,1,64]{2,1,0:T(1,128)} %broadcast_in_dim.110), calls=%async_computation.32 | async-start | bytes 65536 | tf_op jit(solution)/shard_map/all_to_all | solution.py:17
  543.0 8.6 %all-to-all-done.32 = f32[64,1,64]{2,1,0:T(1,128)S(1)} async-done(((f32[64,1,64]{2,1,0:T(1,128)}), f32[64,1,64]{2,1,0:T(1,128)S(1)}, u32[]{:S(2)}, u32[]{:S(2)}) %all-to-all-start.32) | async-done | bytes 16416 | tf_op jit(solution)/shard_map/all_to_all | solution.py:17
  552.3 10.2 %all_to_all.260 = f32[8,1,4096]{2,1,0:T(1,128)S(1)} all-to-all(f32[8,1,4096]{2,1,0:T(1,128)S(1)} %broadcast_in_dim.111), channel_id=1, replica_groups=mesh['dp'=64,'rank'=8] {'rank'}, dimensions={0} | all-to-all | bytes 262144 | tf_op jit(solution)/shard_map/all_to_all | solution.py:17
  563.5 14.8 %all_to_all.261 = f32[64,1,64]{2,1,0:T(1,128)S(1)} all-to-all(f32[64,1,64]{2,1,0:T(1,128)S(1)} %broadcast_in_dim.112), channel_id=1, replica_groups=mesh['dp'=64,'rank'=8] {'dp'}, dimensions={0} | all-to-all | bytes 32768 | tf_op jit(solution)/shard_map/all_to_all | solution.py:17
  579.1 10.2 %all_to_all.262 = f32[8,1,4096]{2,1,0:T(1,128)S(1)} all-to-all(f32[8,1,4096]{2,1,0:T(1,128)S(1)} %broadcast_in_dim.113), channel_id=1, replica_groups=mesh['dp'=64,'rank'=8] {'rank'}, dimensions={0} | all-to-all | bytes 262144 | tf_op jit(solution)/shard_map/all_to_all | solution.py:17
  590.2 15.1 %all_to_all.263 = f32[64,1,64]{2,1,0:T(1,128)S(1)} all-to-all(f32[64,1,64]{2,1,0:T(1,128)S(1)} %broadcast_in_dim.114), channel_id=1, replica_groups=mesh['dp'=64,'rank'=8] {'dp'}, dimensions={0} | all-to-all | bytes 32768 | tf_op jit(solution)/shard_map/all_to_all | solution.py:17
  606.0 10.2 %all_to_all.264 = f32[8,1,4096]{2,1,0:T(1,128)S(1)} all-to-all(f32[8,1,4096]{2,1,0:T(1,128)S(1)} %broadcast_in_dim.115), channel_id=1, replica_groups=mesh['dp'=64,'rank'=8] {'rank'}, dimensions={0} | all-to-all | bytes 262144 | tf_op jit(solution)/shard_map/all_to_all | solution.py:17
  617.2 14.8 %all_to_all.265 = f32[64,1,64]{2,1,0:T(1,128)S(1)} all-to-all(f32[64,1,64]{2,1,0:T(1,128)S(1)} %broadcast_in_dim.116), channel_id=1, replica_groups=mesh['dp'=64,'rank'=8] {'dp'}, dimensions={0} | all-to-all | bytes 32768 | tf_op jit(solution)/shard_map/all_to_all | solution.py:17
  (295 shorter events, 60.2 us)
Async XLA Ops:
  0.6 44.2 %copy-start.5 = (f32[2048]{0:T(1024)S(1)}, f32[2048]{0:T(1024)}, u32[]{:S(2)}) copy-start(f32[2048]{0:T(1024)} %param.10) | copy-start | bytes 24580
  0.6 44.2 %copy-start.4 = (f32[2048]{0:T(1024)S(1)}, f32[2048]{0:T(1024)}, u32[]{:S(2)}) copy-start(f32[2048]{0:T(1024)} %param.9) | copy-start | bytes 24580
  0.7 44.2 %copy-start.1 = (f32[32,2048]{1,0:T(8,128)S(1)}, f32[32,2048]{1,0:T(8,128)}, u32[]{:S(2)}) copy-start(f32[32,2048]{1,0:T(8,128)} %param.11) | copy-start | bytes 786436
  0.7 44.5 %copy-start = (f32[32,2048]{1,0:T(8,128)S(1)}, f32[32,2048]{1,0:T(8,128)}, u32[]{:S(2)}) copy-start(f32[32,2048]{1,0:T(8,128)} %param.12) | copy-start | bytes 786436
  0.7 59.9 %copy-start.6 = (f32[32]{0:T(128)S(1)}, f32[32]{0:T(128)}, u32[]{:S(2)}) copy-start(f32[32]{0:T(128)} %param.13) | copy-start | bytes 388
  5.3 20.9 %all-to-all-start = ((f32[64,1,2]{2,1,0:T(1,128)}), f32[64,1,2]{2,1,0:T(1,128)S(1)}, u32[]{:S(2)}, u32[]{:S(2)}) async-start(f32[64,1,2]{2,1,0:T(1,128)} %broadcast_in_dim.78), calls=%async_computation | async-start | bytes 65536 | tf_op jit(solution)/shard_map/all_to_all | solution.py:17
  26.9 17.8 %all-to-all-start.1 = ((f32[8,1,4096]{2,1,0:T(1,128)}), f32[8,1,4096]{2,1,0:T(1,128)S(1)}, u32[]{:S(2)}, u32[]{:S(2)}) async-start(f32[8,1,4096]{2,1,0:T(1,128)} %broadcast_in_dim.79), calls=%async_computation.1 | async-start | bytes 262144 | tf_op jit(solution)/shard_map/all_to_all | solution.py:17
  88.1 30.9 %copy-start.2 = (f32[64,2048]{1,0:T(8,128)S(1)}, f32[64,2048]{1,0:T(8,128)}, u32[]{:S(2)}) copy-start(f32[64,2048]{1,0:T(8,128)} %param.7) | copy-start | bytes 1572868
  114.5 19.9 %copy-start.3 = (f32[64,2048]{1,0:T(8,128)S(1)}, f32[64,2048]{1,0:T(8,128)}, u32[]{:S(2)}) copy-start(f32[64,2048]{1,0:T(8,128)} %param.8) | copy-start | bytes 1572868
  115.6 11.1 %all-to-all-start.7 = ((f32[8,1,4096]{2,1,0:T(1,128)}), f32[8,1,4096]{2,1,0:T(1,128)S(1)}, u32[]{:S(2)}, u32[]{:S(2)}) async-start(f32[8,1,4096]{2,1,0:T(1,128)} %broadcast_in_dim.85), calls=%async_computation.7 | async-start | bytes 262144 | tf_op jit(solution)/shard_map/all_to_all | solution.py:17
  128.2 15.5 %all-to-all-start.8 = ((f32[64,1,64]{2,1,0:T(1,128)}), f32[64,1,64]{2,1,0:T(1,128)S(1)}, u32[]{:S(2)}, u32[]{:S(2)}) async-start(f32[64,1,64]{2,1,0:T(1,128)} %broadcast_in_dim.86), calls=%async_computation.8 | async-start | bytes 65536 | tf_op jit(solution)/shard_map/all_to_all | solution.py:17
  208.6 17.7 %all-to-all-start.12 = ((f32[64,1,64]{2,1,0:T(1,128)}), f32[64,1,64]{2,1,0:T(1,128)S(1)}, u32[]{:S(2)}, u32[]{:S(2)}) async-start(f32[64,1,64]{2,1,0:T(1,128)} %broadcast_in_dim.90), calls=%async_computation.12 | async-start | bytes 65536 | tf_op jit(solution)/shard_map/all_to_all | solution.py:17
  371.2 17.7 %all-to-all-start.22 = ((f32[64,1,64]{2,1,0:T(1,128)}), f32[64,1,64]{2,1,0:T(1,128)S(1)}, u32[]{:S(2)}, u32[]{:S(2)}) async-start(f32[64,1,64]{2,1,0:T(1,128)} %broadcast_in_dim.100), calls=%async_computation.22 | async-start | bytes 65536 | tf_op jit(solution)/shard_map/all_to_all | solution.py:17
  533.8 17.7 %all-to-all-start.32 = ((f32[64,1,64]{2,1,0:T(1,128)}), f32[64,1,64]{2,1,0:T(1,128)S(1)}, u32[]{:S(2)}, u32[]{:S(2)}) async-start(f32[64,1,64]{2,1,0:T(1,128)} %broadcast_in_dim.110), calls=%async_computation.32 | async-start | bytes 65536 | tf_op jit(solution)/shard_map/all_to_all | solution.py:17
where the time goes:
time: 645 us; the launch traced here: 635 us
  blocking collectives  449 us (70%)
  starting transfers between devices  56.7 us (9%)
  waiting for transfers between devices  55.2 us (9%)
  matrix products  28.6 us (4%)
  other arithmetic  23.6 us (4%)
  local copies, waits for them, and re-layouts  11.9 us (2%)
  between operations  9.37 us (1%)
    all_to_all x32, blocking collectives, from_everyone(): lax.all_to_all(jnp.broadcast_to(value[None], (length, *value.shape)), axi...  449 us
    all_to_all x7, starting transfers between devices, from_everyone(): lax.all_to_all(jnp.broadcast_to(value[None], (length, *value.shape)), axi...  56.7 us
    all_to_all x7, waiting for transfers between devices, from_everyone(): lax.all_to_all(jnp.broadcast_to(value[None], (length, *value.shape)), axi...  55.2 us
  transfers between devices with their start and end apart: 7, of which 7 were waited for; matrix products, arithmetic and copies ran while one was open for 0% of the time, Pallas kernels for 0%

commit v1 on v0

v1 whole, which is shorter than its diff:
```python
import functools

import jax
import jax.numpy as jnp
from jax import lax
from jax.experimental import pallas as pl
from jax.experimental.pallas import tpu as pltpu
from jax.sharding import PartitionSpec as P

RANK = 256
INNER = 4
MIRROR = 3
STEP = 2.0
MESH = pl.DeviceIdType.MESH
EXACT = lax.Precision.HIGHEST

NX, NY, NC, NZ = 4, 8, 2, 8
NDP = NX * NY * NC


def far_first(n):
    return sorted(range(n), key=lambda d: -min(d, n - d))


DP_OFFSETS = sorted(
    [(dx, dy, dc) for dx in range(NX) for dy in range(NY) for dc in range(NC) if (dx, dy, dc) != (0, 0, 0)],
    key=lambda o: -(min(o[0], NX - o[0]) + min(o[1], NY - o[1])),
)
XC_OFFSETS = [o for o in DP_OFFSETS if o[1] == 0]
Y_OFFSETS = [o for o in DP_OFFSETS if o[0] == 0 and o[2] == 0]
Z_OFFSETS = [d for d in far_first(NZ) if d]


def cube_root(x):
    y = jnp.exp2(jnp.log2(x) * (1.0 / 3.0))
    y = y - (y - x / (y * y)) * (1.0 / 3.0)
    return jnp.where(x > 0.0, y, 0.0)


def kernel(
    total_count,
    x_ref, y_ref, mx_ref, my_ref, left_ref, right_ref, w_ref,
    lo_ref, ro_ref, wo_ref,
    k_s, uk_s, xy_s, a_s, n2_s, u_s, vb_s, v_s, k3_s, sc_s, s_s, g_s, c_s,
    zbuf, cbuf, xbuf, ybuf, mbuf,
    zsend, zrecv, csend, crecv, xsend, xrecv, ysend, yrecv, msend, mrecv,
):
    dp = lax.axis_index("dp")
    z = lax.axis_index("rank")
    core = lax.rem(dp, NC)
    yy = lax.rem(lax.div(dp, NC), NY)
    xx = lax.div(dp, NC * NY)
    xc = xx * NC + core
    tiles = left_ref.shape[1] // 128

    def dp_target(o):
        tx = lax.rem(xx + o[0], NX)
        ty = lax.rem(yy + o[1], NY)
        tc = lax.rem(core + o[2], NC)
        return ((tx * NY + ty) * NC + tc, z)

    def z_target(d):
        return (dp, lax.rem(z + d, NZ))

    barrier = pltpu.get_barrier_semaphore()
    for d in Z_OFFSETS:
        pl.semaphore_signal(barrier, inc=1, device_id=z_target(d), device_id_type=MESH)
    for o in DP_OFFSETS:
        pl.semaphore_signal(barrier, inc=1, device_id=dp_target(o), device_id_type=MESH)

    def send(slot, targets, ssem, rsem):
        for t in targets:
            pltpu.make_async_remote_copy(
                src_ref=slot, dst_ref=slot, send_sem=ssem, recv_sem=rsem, device_id=t, device_id_type=MESH
            ).start()

    def wait(some, ssem, rsem):
        pltpu.make_async_copy(some, some, rsem).wait()
        pltpu.make_async_copy(some, some, ssem).wait()

    k_s[0:32, :] = left_ref[...]
    k_s[32:64, :] = right_ref[...]
    xy_s[0:64, :] = x_ref[...]
    xy_s[64:128, :] = y_ref[...]
    a_s[0:tiles, :] = mx_ref[...]
    a_s[tiles:2 * tiles, :] = my_ref[...]
    for t in range(tiles):
        bx = xy_s[0:64, t * 128:(t + 1) * 128]
        by = xy_s[64:128, t * 128:(t + 1) * 128]
        n2_s[t:t + 1, :] = jnp.sum(bx * bx, axis=0, keepdims=True)
        n2_s[tiles + t:tiles + t + 1, :] = jnp.sum(by * by, axis=0, keepdims=True)
    k3_s[...] = w_ref[...]
    sc_s[...] = jnp.ones((1, 128), jnp.float32)
    lane = lax.broadcasted_iota(jnp.int32, (1, 128), 1)
    pl.semaphore_wait(barrier, len(Z_OFFSETS) + len(DP_OFFSETS))

    def spread(vec):
        return jnp.broadcast_to(vec, (128, 128)).T

    def gather_rows(rows):
        return jnp.sum(rows.T, axis=0, keepdims=True)

    def doubled(c):
        return jnp.where(lane < 64, c, pltpu.roll(c, 64, 1))

    def row_sums(par):
        for t in range(tiles):
            b = k_s[:, t * 128:(t + 1) * 128] * vb_s[...]
            zbuf[par, z, t:t + 1, :] = jnp.sum(b[0:32], axis=0, keepdims=True)
            zbuf[par, z, tiles + t:tiles + t + 1, :] = jnp.sum(b[32:64], axis=0, keepdims=True)
        send(zbuf.at[par, z], [z_target(d) for d in Z_OFFSETS], zsend.at[par], zrecv.at[par])
        wait(zbuf.at[par, 0:NZ - 1], zsend.at[par], zrecv.at[par])
        total = zbuf[par, 0]
        for i in range(1, NZ):
            total = total + zbuf[par, i]
        u_s[...] = a_s[...] / total

    def column_parts(weights):
        accs = [jnp.zeros((64, 128), jnp.float32) for _ in weights]
        for t in range(tiles):
            b = k_s[:, t * 128:(t + 1) * 128]
            for j, w in enumerate(weights):
                wl = jnp.broadcast_to(w[t:t + 1, :], (32, 128))
                wr = jnp.broadcast_to(w[tiles + t:tiles + t + 1, :], (32, 128))
                accs[j] = accs[j] + b * jnp.concatenate([wl, wr], axis=0)
        return accs

    def start_columns(par, low, high):
        cbuf[par, dp] = gather_rows(jnp.concatenate([low, high], axis=0))
        send(cbuf.at[par, dp], [dp_target(o) for o in DP_OFFSETS], csend.at[par], crecv.at[par])

    def end_columns(par):
        wait(cbuf.at[par, 0:NDP - 1], csend.at[par], crecv.at[par])
        parts = [cbuf[par, i] for i in range(4)]
        for i in range(4, NDP):
            parts[i % 4] = parts[i % 4] + cbuf[par, i]
        return (parts[0] + parts[1]) + (parts[2] + parts[3])

    def rescale(c):
        v = v_s[...]
        p = v * c
        g = cube_root(k3_s[...] * p * pltpu.roll(p, 32, 1))
        v = g / c
        v_s[...] = v
        g_s[...] = g
        return v

    def plain_step(step):
        par = lax.rem(step, 2)
        row_sums(par)
        (low,) = column_parts([u_s])
        half = tiles
        ax = jnp.sum(a_s[0:half, :], axis=0, keepdims=True)
        ay = jnp.sum(a_s[half:2 * half, :], axis=0, keepdims=True)
        high = jnp.concatenate([jnp.broadcast_to(ax, (32, 128)), jnp.broadcast_to(ay, (32, 128))], axis=0)
        start_columns(par, low, high)
        c = end_columns(par)
        mass = jnp.where(lane >= 64, c, pltpu.roll(c, 64, 1))
        scale = total_count / mass
        sc_s[...] = scale
        v = rescale(doubled(c) * scale)
        vb_s[...] = spread(v)[0:64]

    def last_step(step, moments):
        par = lax.rem(step, 2)
        row_sums(par)
        if moments:
            for t in range(tiles):
                n2_s[2 * tiles + t:2 * tiles + t + 1, :] = u_s[t:t + 1, :] * n2_s[t:t + 1, :]
                n2_s[3 * tiles + t:3 * tiles + t + 1, :] = u_s[tiles + t:tiles + t + 1, :] * n2_s[tiles + t:tiles + t + 1, :]
            low, high = column_parts([u_s, n2_s.at[2 * tiles:4 * tiles]])
        else:
            (low,) = column_parts([u_s])
            high = low
        start_columns(par, low, high)
        for t in range(tiles):
            cols = slice(t * 128, (t + 1) * 128)
            uk_s[0:32, cols] = k_s[0:32, cols] * jnp.broadcast_to(u_s[t:t + 1, :], (32, 128))
            uk_s[32:64, cols] = k_s[32:64, cols] * jnp.broadcast_to(u_s[tiles + t:tiles + t + 1, :], (32, 128))
        if moments:
            both = lax.dot_general(
                uk_s[...], xy_s[...], (((1,), (1,)), ((), ())),
                precision=EXACT, preferred_element_type=jnp.float32,
            )
            xbuf[xc] = jnp.where(lane < 64, both[0:32], both[32:64])
            send(xbuf.at[xc], [dp_target(o) for o in XC_OFFSETS], xsend, xrecv)
        c = end_columns(par)
        scale = sc_s[...]
        cn = doubled(c) * scale
        v = rescale(cn)
        return c, cn, v, v * scale

    def projection(base, moments):
        v_s[...] = jnp.ones((1, 128), jnp.float32)
        vb_s[...] = jnp.ones((64, 128), jnp.float32)

        def body(t, carry):
            plain_step(base + t)
            return carry

        lax.fori_loop(0, INNER - 1, body, 0)
        return last_step(base + (INNER - 1), moments)

    def mirror(outer, carry):
        c, cn, v, veff = projection(outer * INNER, True)
        g = g_s[...]
        wait(xbuf.at[0:NX * NC - 1], xsend, xrecv)
        m = xbuf[0]
        for i in range(1, NX * NC):
            m = m + xbuf[i]
        ybuf[yy] = m
        send(ybuf.at[yy], [dp_target(o) for o in Y_OFFSETS], ysend, yrecv)
        sq = jnp.where(lane < 64, pltpu.roll(c, 64, 1), c) * veff
        qs = cn * v
        cross = sq * pltpu.roll(qs, 32, 1)
        cross = cross + pltpu.roll(cross, 32, 1)
        hh = pltpu.roll(sq, 32, 1) / g
        swapped = pltpu.roll(veff, 32, 1)
        wait(ybuf.at[0:NY - 1], ysend, yrecv)
        m = ybuf[0]
        for i in range(1, NY):
            m = m + ybuf[i]
        turned = pltpu.roll(m, 64, 1)
        prod = m * turned
        dots = jnp.sum(jnp.concatenate([prod] * 4, axis=0).T[0:64], axis=0, keepdims=True)
        gg = -(cross - 2.0 * dots * veff * swapped) / (g * g)
        mbuf[z] = jnp.where(lane < 64, hh, jnp.where(lane < 96, gg, 0.0))
        send(mbuf.at[z], [z_target(d) for d in Z_OFFSETS], msend, mrecv)
        factor = spread(swapped * (2.0 * STEP) / g)[0:64]
        wide = lax.broadcasted_iota(jnp.int32, (32, 128), 1)
        w = jnp.concatenate([jnp.where(wide < 64, turned, 0.0), jnp.where(wide < 64, 0.0, turned)], axis=0) * factor
        qv = spread(veff)[0:64]
        wait(mbuf.at[0:NZ - 1], msend, mrecv)
        s = mbuf[0]
        for i in range(1, NZ):
            s = s + mbuf[i]
        mq = jnp.sum(jnp.where(lane < 32, s, 0.0), axis=1, keepdims=True) / RANK
        mr = jnp.sum(jnp.where((lane >= 32) & (lane < 64), s, 0.0), axis=1, keepdims=True) / RANK
        mg = jnp.sum(jnp.where((lane >= 64) & (lane < 96), s, 0.0), axis=1, keepdims=True) / RANK
        mean = jnp.where(lax.rem(lane, 64) < 32, mq, mr)
        shift = spread((hh - mean) * (-STEP))[0:64]
        k3_s[...] = g * jnp.exp(-STEP * (gg - mg))
        for t in range(tiles // 2):
            cols = slice(t * 256, (t + 1) * 256)
            f = lax.dot_general(
                w, xy_s[:, cols], (((1,), (0,)), ((), ())),
                precision=EXACT, preferred_element_type=jnp.float32,
            )
            sh = jnp.concatenate([shift, shift], axis=1)
            q2 = jnp.concatenate([qv, qv], axis=1)
            k_s[:, cols] = uk_s[:, cols] * q2 * jnp.exp(f + sh)
        return carry

    lax.fori_loop(0, MIRROR, mirror, 0)
    _, _, v, veff = projection(MIRROR * INNER, False)
    qv = spread(veff * RANK)[0:64]
    for t in range(tiles):
        cols = slice(t * 128, (t + 1) * 128)
        out = uk_s[:, cols] * qv
        lo_ref[:, cols] = out[0:32]
        ro_ref[:, cols] = out[32:64]
    wo_ref[...] = g_s[...] * (RANK / total_count)


def shards(cloud_x, cloud_y, mass_x, mass_y, left_start, right_start, weight_start):
    ranks, points = left_start.shape
    total_count = float(points * lax.axis_size("dp"))
    tiles = points // 128
    f32 = jnp.float32
    dma = pltpu.SemaphoreType.DMA
    left, right, weights = pl.pallas_call(
        functools.partial(kernel, total_count),
        name="sinkhorn",
        out_shape=(
            jax.ShapeDtypeStruct((ranks, points), f32),
            jax.ShapeDtypeStruct((ranks, points), f32),
            jax.ShapeDtypeStruct((1, 128), f32),
        ),
        in_specs=[pl.BlockSpec(memory_space=pltpu.VMEM)] * 7,
        out_specs=[pl.BlockSpec(memory_space=pltpu.VMEM)] * 3,
        scratch_shapes=[
            pltpu.VMEM((2 * ranks, points), f32),
            pltpu.VMEM((2 * ranks, points), f32),
            pltpu.VMEM((128, points), f32),
            pltpu.VMEM((2 * tiles, 128), f32),
            pltpu.VMEM((4 * tiles, 128), f32),
            pltpu.VMEM((2 * tiles, 128), f32),
            pltpu.VMEM((64, 128), f32),
            pltpu.VMEM((1, 128), f32),
            pltpu.VMEM((1, 128), f32),
            pltpu.VMEM((1, 128), f32),
            pltpu.VMEM((1, 128), f32),
            pltpu.VMEM((1, 128), f32),
            pltpu.VMEM((1, 128), f32),
            pltpu.VMEM((2, NZ, 2 * tiles, 128), f32),
            pltpu.VMEM((2, NDP, 1, 128), f32),
            pltpu.VMEM((NX * NC, 32, 128), f32),
            pltpu.VMEM((NY, 32, 128), f32),
            pltpu.VMEM((NZ, 1, 128), f32),
            dma((2,)), dma((2,)), dma((2,)), dma((2,)),
            dma, dma, dma, dma, dma, dma,
        ],
        compiler_params=pltpu.CompilerParams(collective_id=0, has_side_effects=True),
    )(
        cloud_x, cloud_y, mass_x.reshape(tiles, 128), mass_y.reshape(tiles, 128),
        left_start, right_start, jnp.tile(weight_start, 4)[None],
    )
    return left, right, weights[0, :ranks]


def solution(mesh):
    in_specs = (
        P(None, "dp"),
        P(None, "dp"),
        P("dp"),
        P("dp"),
        P("rank", "dp"),
        P("rank", "dp"),
        P("rank"),
    )
    out_specs = (P("rank", "dp"), P("rank", "dp"), P("rank"))
    return jax.shard_map(shards, mesh=mesh, in_specs=in_specs, out_specs=out_specs, check_vma=False)
```

time: 645 us -> 244 us (0.38); the launches traced: 635 us -> 244 us
  blocking collectives: 449 us -> 0 us
  Pallas kernels: 0 us -> 238 us
  starting transfers between devices: 56.7 us -> 0 us
  waiting for transfers between devices: 55.2 us -> 0 us
  matrix products: 28.6 us -> 0 us
  other arithmetic: 23.6 us -> 0 us
  between operations: 9.37 us -> 0.66 us
  local copies, waits for them, and re-layouts: 11.9 us -> 4.76 us
    all_to_all x32 -> x0, blocking collectives: 449 us -> none  [from_everyone(): lax.all_to_all(jnp.broadcast_to(value[None], (length, *value.shape)), axi...]
    pallas_call x0 -> x1, Pallas kernels: none -> 238 us  [shards(): pl.pallas_call(functools.partial(kernel, total_count), name='sinkhorn', o...]
    all_to_all x7 -> x0, starting transfers between devices: 56.7 us -> none  [from_everyone(): lax.all_to_all(jnp.broadcast_to(value[None], (length, *value.shape)), axi...]
    all_to_all x7 -> x0, waiting for transfers between devices: 55.2 us -> none  [from_everyone(): lax.all_to_all(jnp.broadcast_to(value[None], (length, *value.shape)), axi...]
    dot_general x82 -> x0, matrix products: 28.6 us -> none  [the longest x16 5.42 us: project(): jnp.dot(scale_right, kernel_right, precision=exact_mode)]
    reduce_sum x54 -> x0, other arithmetic: 10.4 us -> none  [the longest x39 4.12 us: of_everyone(): return from_everyone(value, axis).sum(axis=0)]
    concatenate x36 -> x0, other arithmetic: 9.35 us -> none  [in_one(): total = of_everyone(jnp.concatenate([a.ravel() for a in arrays]), axis)]
    broadcast_in_dim x39 -> x0, local copies, waits for them, and re-layouts: 7.66 us -> none  [from_everyone(): jnp.broadcast_to(value[None], (length, *value.shape))]
  transfers between devices with their start and end apart: 7 -> 0, of which waited for: 7 -> 0; matrix products, arithmetic and copies ran while one was open for 0% -> 0% of each run, Pallas kernels for 0% -> 0%
where the time goes in v1:
time: 244 us
  Pallas kernels  238 us (98%)
  local copies, waits for them, and re-layouts  4.76 us (2%)
    pallas_call x1, Pallas kernels, shards(): pl.pallas_call(functools.partial(kernel, total_count), name='sinkhorn', o...  238 us

profile of v1, /device:TPU:1, one launch (start us, length us, event | category | flops | bytes accessed | tf_op | source)
XLA Modules:
  0.0 243.6 jit_solution(33138778179004359)
XLA Ops:
  0.6 0.0 copy-start.1
  0.6 0.6 copy-done.1
  1.3 0.6 broadcast_in_dim_tile.3.w_ref
  1.9 238.2 %sinkhorn.1 = (f32[32,2048]{1,0:T(8,128)}, f32[32,2048]{1,0:T(8,128)}, f32[1,128]{1,0:T(1,128)}) custom-call(f32[64,2048]{1,0:T(8,128)} %x_ref.1, f32[64,2048]{1,0:T(8,128)} %y_ref.1, f32[16,128]{1,0:T(8,128)} %bitcast.4, f32[16,128]{1,0:T(8,128)} %bitcast.5, f32[32,2048]{1,0:T(8,128)} %left_ref.1, f32[32,2048]{1,0:T(8,128)} %right_ref.1, ...), custom_call_target="tpu_custom_call" | custom-call | tf_op jit(solution)/shard_map/sinkhorn/pallas_call | solution.py:271
  240.1 0.0 copy-start.2
  240.1 0.6 copy-done.2
  240.7 0.5 slice_bitcast_fusion
  241.2 0.0 copy-start
  241.2 1.7 copy.12
  242.9 0.0 copy-done
  242.9 0.7 copy.13
  (1 shorter events, 0.0 us)
Async XLA Ops:
  0.6 0.7 copy-start.1
  240.1 0.6 copy-start.2
  241.2 1.7 copy-start

commit v2 on v1

v2 whole, which is shorter than its diff:
```python
import functools

import jax
import jax.numpy as jnp
from jax import lax
from jax.experimental import pallas as pl
from jax.experimental.pallas import tpu as pltpu
from jax.sharding import PartitionSpec as P

RANK = 256
INNER = 4
MIRROR = 3
STEP = 2.0
MESH = pl.DeviceIdType.MESH
EXACT = lax.Precision.HIGHEST
LOG2E = 1.4426950408889634

NX, NY, NC, NZ = 4, 8, 2, 8
NDP = NX * NY * NC


def far_first(n):
    return sorted(range(n), key=lambda d: -min(d, n - d))


DP_OFFSETS = sorted(
    [(dx, dy, dc) for dx in range(NX) for dy in range(NY) for dc in range(NC) if (dx, dy, dc) != (0, 0, 0)],
    key=lambda o: -(min(o[0], NX - o[0]) + min(o[1], NY - o[1])),
)
XC_OFFSETS = [o for o in DP_OFFSETS if o[1] == 0]
Y_OFFSETS = [o for o in DP_OFFSETS if o[0] == 0 and o[2] == 0]
Z_OFFSETS = [d for d in far_first(NZ) if d]


def cube_root(x):
    y = jnp.exp2(jnp.log2(x) * (1.0 / 3.0))
    y = y - (y - x / (y * y)) * (1.0 / 3.0)
    return jnp.where(x > 0.0, y, 0.0)


def split(x):
    high = x.astype(jnp.bfloat16)
    return high, (x - high.astype(jnp.float32)).astype(jnp.bfloat16)


def kernel(
    total_count,
    x_ref, y_ref, mx_ref, my_ref, left_ref, right_ref, w_ref,
    lo_ref, ro_ref, wo_ref,
    k_s, c_s, uk_s, xy_s, x4_s, w4_s, a_s, n2_s, u_s, vb_s, fb_s, sb_s,
    v1_s, k1_s, sc_s, v_s, k3_s, g_s, veff_s, qs_s,
    zbuf, cbuf, dbuf, xbuf, ybuf, mbuf,
    zsend, zrecv, csend, crecv, dsend, drecv, xsend, xrecv, ysend, yrecv, msend, mrecv, asend, arecv,
):
    dp = lax.axis_index("dp")
    z = lax.axis_index("rank")
    core = lax.rem(dp, NC)
    yy = lax.rem(lax.div(dp, NC), NY)
    xx = lax.div(dp, NC * NY)
    xc = xx * NC + core
    tiles = left_ref.shape[1] // 128
    half = left_ref.shape[0]

    def dp_target(o):
        tx = lax.rem(xx + o[0], NX)
        ty = lax.rem(yy + o[1], NY)
        tc = lax.rem(core + o[2], NC)
        return ((tx * NY + ty) * NC + tc, z)

    def z_target(d):
        return (dp, lax.rem(z + d, NZ))

    barrier = pltpu.get_barrier_semaphore()
    for d in Z_OFFSETS:
        pl.semaphore_signal(barrier, inc=1, device_id=z_target(d), device_id_type=MESH)
    for o in DP_OFFSETS:
        pl.semaphore_signal(barrier, inc=1, device_id=dp_target(o), device_id_type=MESH)

    def send(slot, targets, ssem, rsem):
        for t in targets:
            pltpu.make_async_remote_copy(
                src_ref=slot, dst_ref=slot, send_sem=ssem, recv_sem=rsem, device_id=t, device_id_type=MESH
            ).start()

    def wait(some, ssem, rsem):
        pltpu.make_async_copy(some, some, rsem).wait()
        pltpu.make_async_copy(some, some, ssem).wait()

    def tile(t):
        return slice(t * 128, (t + 1) * 128)

    k_s[z, 0:half, :] = left_ref[...]
    k_s[z, half:2 * half, :] = right_ref[...]
    xy_s[0:64, :] = x_ref[...]
    xy_s[64:128, :] = y_ref[...]
    a_s[0:tiles, :] = mx_ref[...]
    a_s[tiles:2 * tiles, :] = my_ref[...]
    lane = lax.broadcasted_iota(jnp.int32, (1, 128), 1)
    wide = lax.broadcasted_iota(jnp.int32, (4, 128), 1)
    pl.semaphore_wait(barrier, len(Z_OFFSETS) + len(DP_OFFSETS))

    def spread(vec):
        return jnp.broadcast_to(vec, (128, 128)).T

    def spread_all(dst, packed):
        for r in range(4):
            s = spread(packed[r:r + 1])
            dst[r] = s[0:64]
            dst[r + 4] = s[64:128]

    def gather_rows(rows):
        return jnp.sum(rows.T, axis=0, keepdims=True)

    def swap(p):
        return jnp.where(lax.rem(lax.broadcasted_iota(jnp.int32, p.shape, 1), 64) < 32, pltpu.roll(p, 96, 1), pltpu.roll(p, 32, 1))

    def doubled(c):
        return jnp.where(lane < 64, c, pltpu.roll(c, 64, 1))

    def packed(rows):
        return jnp.concatenate([jnp.where(lane < 64, rows[r], rows[r + 4]) for r in range(4)], axis=0)

    def ring(hop, go):
        for way, sign in ((0, 1), (1, -1)):
            block = lax.rem(z - sign * hop + NZ, NZ)
            part = k_s.at[block]
            if hop == NZ // 2 - 1:
                part = k_s.at[block, half * way:half * (way + 1)]
            copy = pltpu.make_async_remote_copy(
                src_ref=part, dst_ref=part, send_sem=asend.at[hop, way], recv_sem=arecv.at[hop, way],
                device_id=(dp, lax.rem(z + sign + NZ, NZ)), device_id_type=MESH,
            )
            if go:
                copy.start()
            else:
                copy.wait_recv()
                copy.wait_send()

    def ring_step(step):
        for hop in range(NZ // 2):
            @pl.when(step == hop)
            def _():
                if hop:
                    ring(hop - 1, False)
                ring(hop, True)

    def row_sums(step):
        par = lax.rem(step, 2)
        for t in range(tiles):
            b = k_s[z, :, tile(t)] * vb_s[0]
            zbuf[par, z, t:t + 1, :] = jnp.sum(b[0:half], axis=0, keepdims=True)
            zbuf[par, z, tiles + t:tiles + t + 1, :] = jnp.sum(b[half:2 * half], axis=0, keepdims=True)
        send(zbuf.at[par, z], [z_target(d) for d in Z_OFFSETS], zsend.at[par], zrecv.at[par])
        ring_step(step)

        @pl.when(step == 0)
        def _():
            prepare()

        wait(zbuf.at[par, 0:NZ - 1], zsend.at[par], zrecv.at[par])
        total = zbuf[par, 0]
        for i in range(1, NZ):
            total = total + zbuf[par, i]
        u_s[...] = a_s[...] / total

    def prepare():
        for t in range(tiles):
            bx = xy_s[0:64, tile(t)]
            by = xy_s[64:128, tile(t)]
            n2_s[t:t + 1, :] = jnp.sum(bx * bx, axis=0, keepdims=True)
            n2_s[tiles + t:tiles + t + 1, :] = jnp.sum(by * by, axis=0, keepdims=True)
            for i, b in enumerate((bx, by)):
                high, low = split(b)
                both = jnp.concatenate([high, low], axis=0)
                x4_s[i, 0:128, tile(t)] = both
                x4_s[i, 128:256, tile(t)] = both

    def own_parts(w):
        acc = jnp.zeros((64, 128), jnp.float32)
        for t in range(tiles):
            wl = jnp.broadcast_to(w[t:t + 1, :], (half, 128))
            wr = jnp.broadcast_to(w[tiles + t:tiles + t + 1, :], (half, 128))
            acc = acc + k_s[z, :, tile(t)] * jnp.concatenate([wl, wr], axis=0)
        return acc

    def exchange_columns(par):
        send(cbuf.at[par, dp], [dp_target(o) for o in DP_OFFSETS], csend.at[par], crecv.at[par])

    def summed(buf, par):
        parts = [buf[par, i] for i in range(4)]
        for i in range(4, NDP):
            parts[i % 4] = parts[i % 4] + buf[par, i]
        return (parts[0] + parts[1]) + (parts[2] + parts[3])

    def rescale(c, v_ref, k_ref):
        v = v_ref[...]
        p = v * c
        g = cube_root(k_ref[...] * p * swap(p))
        v = g / c
        v_ref[...] = v
        return g, v

    def first_step(step, carry):
        par = lax.rem(step, 2)
        row_sums(step)
        low = own_parts(u_s)
        ax = jnp.sum(a_s[0:tiles, :], axis=0, keepdims=True)
        ay = jnp.sum(a_s[tiles:2 * tiles, :], axis=0, keepdims=True)
        high = jnp.concatenate([jnp.broadcast_to(ax, (32, 128)), jnp.broadcast_to(ay, (32, 128))], axis=0)
        cbuf[par, dp] = gather_rows(jnp.concatenate([low, high], axis=0))
        exchange_columns(par)
        wait(cbuf.at[par, 0:NDP - 1], csend.at[par], crecv.at[par])
        c = summed(cbuf, par)
        scale = total_count / jnp.where(lane >= 64, c, pltpu.roll(c, 64, 1))
        sc_s[...] = scale
        g, v = rescale(doubled(c) * scale, v1_s, k1_s)
        vb_s[0] = spread(v)[0:64]
        return carry

    def start_moments():
        for t in range(tiles):
            uk_s[0:half, tile(t)] = k_s[z, 0:half, tile(t)] * jnp.broadcast_to(u_s[t:t + 1, :], (half, 128))
            uk_s[half:2 * half, tile(t)] = k_s[z, half:2 * half, tile(t)] * jnp.broadcast_to(u_s[tiles + t:tiles + t + 1, :], (half, 128))
        acc = jnp.zeros((64, 128), jnp.float32)
        for t in range(tiles):
            nl = jnp.broadcast_to(n2_s[t:t + 1, :], (half, 128))
            nr = jnp.broadcast_to(n2_s[tiles + t:tiles + t + 1, :], (half, 128))
            acc = acc + uk_s[:, tile(t)] * jnp.concatenate([nl, nr], axis=0)
        both = lax.dot_general(
            uk_s[...], xy_s[...], (((1,), (1,)), ((), ())), precision=EXACT, preferred_element_type=jnp.float32
        )
        xbuf[xc, 0:32] = jnp.where(lane < 64, both[0:half], both[half:2 * half])
        xbuf[xc, 32:40] = jnp.broadcast_to(gather_rows(jnp.concatenate([acc, acc], axis=0)), (8, 128))
        send(xbuf.at[xc], [dp_target(o) for o in XC_OFFSETS], xsend, xrecv)

    def middle_moments():
        wait(xbuf.at[0:NX * NC - 1], xsend, xrecv)
        m = xbuf[0]
        for i in range(1, NX * NC):
            m = m + xbuf[i]
        ybuf[yy] = m
        send(ybuf.at[yy], [dp_target(o) for o in Y_OFFSETS], ysend, yrecv)

    def end_moments(par, rows):
        wait(ybuf.at[0:NY - 1], ysend, yrecv)
        m = ybuf[0]
        for i in range(1, NY):
            m = m + ybuf[i]
        mbuf[par, z] = m
        for i, row in enumerate(rows):
            mbuf[par, z, 33 + i:34 + i] = row
        send(mbuf.at[par, z], [z_target(d) for d in Z_OFFSETS], msend.at[par], mrecv.at[par])

    v1_s[...] = jnp.ones((1, 128), jnp.float32)
    k1_s[...] = w_ref[...]
    vb_s[0] = jnp.ones((64, 128), jnp.float32)
    lax.fori_loop(0, INNER - 1, first_step, 0)
    par = (INNER - 1) % 2
    row_sums(INNER - 1)
    start_moments()
    low = own_parts(u_s)
    cbuf[par, dp] = gather_rows(jnp.concatenate([low, low], axis=0))
    exchange_columns(par)
    middle_moments()
    wait(cbuf.at[par, 0:NDP - 1], csend.at[par], crecv.at[par])
    c1 = summed(cbuf, par) * sc_s[...]
    g1, v1 = rescale(c1, v1_s, k1_s)
    end_moments(0, (g1, v1 * sc_s[...], c1 * v1))
    ring(NZ // 2 - 1, False)
    wait(mbuf.at[0, 0:NZ - 1], msend.at[0], mrecv.at[0])
    g_s[...] = packed([mbuf[0, b, 33:34] for b in range(NZ)])
    veff_s[...] = packed([mbuf[0, b, 34:35] for b in range(NZ)])
    qs_s[...] = packed([mbuf[0, b, 35:36] for b in range(NZ)])

    def u_of_rows():
        for side in range(2):
            def body(b, accs):
                accs = list(accs)
                for j in range(half // 8):
                    rows = slice(side * half + 8 * j, side * half + 8 * j + 8)
                    v = vb_s[b, rows]
                    for t in range(tiles):
                        accs[t] = accs[t] + k_s[b, rows, tile(t)] * v
                return tuple(accs)

            accs = lax.fori_loop(0, NZ, body, tuple(jnp.zeros((8, 128), jnp.float32) for _ in range(tiles)))
            for t in range(tiles):
                i = side * tiles + t
                u_s[i:i + 1, :] = a_s[i:i + 1, :] / jnp.sum(accs[t], axis=0, keepdims=True)

    def start_columns(par):
        for side in range(2):
            us = [jnp.broadcast_to(u_s[side * tiles + t:side * tiles + t + 1, :], (8, 128)) for t in range(tiles)]

            def body(b, carry):
                for j in range(half // 8):
                    rows = slice(side * half + 8 * j, side * half + 8 * j + 8)
                    acc = [k_s[b, rows, tile(t)] * us[t] for t in range(tiles)]
                    while len(acc) > 1:
                        acc = [p + q for p, q in zip(acc[::2], acc[1::2])]
                    c_s[b, rows] = acc[0]
                return carry

            lax.fori_loop(0, NZ, body, 0)
        dbuf[par, dp] = jnp.concatenate(
            [gather_rows(jnp.concatenate([c_s[r], c_s[r + 4]], axis=0)) for r in range(4)], axis=0
        )
        send(dbuf.at[par, dp], [dp_target(o) for o in DP_OFFSETS], dsend.at[par], drecv.at[par])

    def end_columns(par):
        wait(dbuf.at[par, 0:NDP - 1], dsend.at[par], drecv.at[par])
        c = summed(dbuf, par) * sc_s[...]
        g, v = rescale(c, v_s, k3_s)
        return c, g, v

    def plain_step(step):
        par = lax.rem(step, 2)
        u_of_rows()
        start_columns(par)
        _, _, v = end_columns(par)
        spread_all(vb_s, v)

    def mirror(outer, carry):
        mpar = lax.rem(outer, 2)
        g = g_s[...]
        veff = veff_s[...]
        qs = qs_s[...]
        sq = packed([mbuf[mpar, b, 32:33] for b in range(NZ)]) * veff
        cross = sq * swap(qs)
        cross = cross + swap(cross)
        other = swap(veff)
        dots = []
        for r in range(4):
            prods = [mbuf[mpar, b, 0:32] * pltpu.roll(mbuf[mpar, b, 0:32], 64, 1) for b in (r, r + 4)]
            rows = jnp.concatenate([prods[0], prods[0], prods[1], prods[1]], axis=0)
            dots.append(jnp.sum(rows.T[0:64], axis=0, keepdims=True))
        gg = -(cross - 2.0 * jnp.concatenate(dots, axis=0) * veff * other) / (g * g)
        hh = swap(sq) / g
        left_lanes = lax.rem(wide, 64) < 32
        total = lambda p: jnp.sum(jnp.sum(p, axis=1, keepdims=True), axis=0, keepdims=True)
        mq = total(jnp.where(left_lanes, hh, 0.0)) / RANK
        mr = total(jnp.where(left_lanes, 0.0, hh)) / RANK
        mg = total(jnp.where(left_lanes, gg, 0.0)) / RANK
        k3_s[...] = g * jnp.exp(-STEP * (gg - mg))
        spread_all(fb_s, other * (2.0 * STEP * LOG2E) / g)
        spread_all(sb_s, (hh - jnp.where(left_lanes, mq, mr)) * (-STEP * LOG2E))
        spread_all(vb_s, veff)
        for b in range(NZ):
            m = mbuf[mpar, b, 0:32]
            turned = pltpu.roll(m, 64, 1)
            for side, first in ((0, turned), (1, m)):
                doubled_m = jnp.where(lane < 64, first, pltpu.roll(first, 64, 1))
                high, low = split(doubled_m * fb_s[b, 32 * side:32 * side + 32])
                w4_s[side, 32 * b:32 * b + 32, 0:128] = high
                w4_s[side, 32 * b:32 * b + 32, 128:256] = low
        for side in range(2):
            for t in range(tiles // 2):
                cols = slice(t * 256, (t + 1) * 256)
                f = jnp.dot(w4_s[side], x4_s[side, :, cols], preferred_element_type=jnp.float32)
                ua = jnp.concatenate(
                    [jnp.broadcast_to(u_s[side * tiles + 2 * t + i:side * tiles + 2 * t + i + 1, :], (32, 128)) for i in range(2)], axis=1
                )
                for b in range(NZ):
                    rows = slice(32 * side, 32 * side + 32)
                    s = sb_s[b, rows]
                    q = vb_s[b, rows]
                    e = jnp.exp2(f[32 * b:32 * b + 32] + jnp.concatenate([s, s], axis=1))
                    k_s[b, rows, cols] = k_s[b, rows, cols] * ua * jnp.concatenate([q, q], axis=1) * e

        v_s[...] = jnp.ones((4, 128), jnp.float32)
        vb_s[...] = jnp.ones((NZ, 64, 128), jnp.float32)
        base = outer * INNER

        def body(t, inner):
            plain_step(base + t)
            return inner

        lax.fori_loop(0, INNER - 1, body, 0)
        step = base + (INNER - 1)
        par = lax.rem(step, 2)
        u_of_rows()

        @pl.when(outer < MIRROR - 1)
        def _():
            start_moments()

        start_columns(par)

        @pl.when(outer < MIRROR - 1)
        def _():
            middle_moments()

        c, g, v = end_columns(par)
        g_s[...] = g
        veff_s[...] = v * sc_s[...]
        qs_s[...] = c * v
        npar = lax.rem(outer + 1, 2)

        @pl.when(outer < MIRROR - 1)
        def _():
            end_moments(npar, ())
            wait(mbuf.at[npar, 0:NZ - 1], msend.at[npar], mrecv.at[npar])

        return carry

    lax.fori_loop(0, MIRROR, mirror, 0)
    spread_all(vb_s, veff_s[...] * RANK)
    qv = vb_s[z]
    for t in range(tiles):
        lo_ref[:, tile(t)] = k_s[z, 0:half, tile(t)] * qv[0:half] * jnp.broadcast_to(u_s[t:t + 1, :], (half, 128))
        ro_ref[:, tile(t)] = k_s[z, half:2 * half, tile(t)] * qv[half:2 * half] * jnp.broadcast_to(
            u_s[tiles + t:tiles + t + 1, :], (half, 128))
    wo_ref[...] = g_s[...] * (RANK / total_count)


def shards(cloud_x, cloud_y, mass_x, mass_y, left_start, right_start, weight_start):
    ranks, points = left_start.shape
    total_count = float(points * lax.axis_size("dp"))
    tiles = points // 128
    f32 = jnp.float32
    bf16 = jnp.bfloat16
    dma = pltpu.SemaphoreType.DMA
    left, right, weights = pl.pallas_call(
        functools.partial(kernel, total_count),
        name="sinkhorn",
        out_shape=(
            jax.ShapeDtypeStruct((ranks, points), f32),
            jax.ShapeDtypeStruct((ranks, points), f32),
            jax.ShapeDtypeStruct((4, 128), f32),
        ),
        in_specs=[pl.BlockSpec(memory_space=pltpu.VMEM)] * 7,
        out_specs=[pl.BlockSpec(memory_space=pltpu.VMEM)] * 3,
        scratch_shapes=[
            pltpu.VMEM((NZ, 2 * ranks, points), f32),
            pltpu.VMEM((NZ, 2 * ranks, 128), f32),
            pltpu.VMEM((2 * ranks, points), f32),
            pltpu.VMEM((128, points), f32),
            pltpu.VMEM((2, 256, points), bf16),
            pltpu.VMEM((2, 256, 256), bf16),
            pltpu.VMEM((2 * tiles, 128), f32),
            pltpu.VMEM((2 * tiles, 128), f32),
            pltpu.VMEM((2 * tiles, 128), f32),
            pltpu.VMEM((NZ, 64, 128), f32),
            pltpu.VMEM((NZ, 64, 128), f32),
            pltpu.VMEM((NZ, 64, 128), f32),
            pltpu.VMEM((1, 128), f32),
            pltpu.VMEM((1, 128), f32),
            pltpu.VMEM((1, 128), f32),
            pltpu.VMEM((4, 128), f32),
            pltpu.VMEM((4, 128), f32),
            pltpu.VMEM((4, 128), f32),
            pltpu.VMEM((4, 128), f32),
            pltpu.VMEM((4, 128), f32),
            pltpu.VMEM((2, NZ, 2 * tiles, 128), f32),
            pltpu.VMEM((2, NDP, 1, 128), f32),
            pltpu.VMEM((2, NDP, 4, 128), f32),
            pltpu.VMEM((NX * NC, 40, 128), f32),
            pltpu.VMEM((NY, 40, 128), f32),
            pltpu.VMEM((2, NZ, 40, 128), f32),
            dma((2,)), dma((2,)), dma((2,)), dma((2,)), dma((2,)), dma((2,)),
            dma, dma, dma, dma, dma((2,)), dma((2,)),
            dma((NZ // 2, 2)), dma((NZ // 2, 2)),
        ],
        compiler_params=pltpu.CompilerParams(collective_id=0, has_side_effects=True),
    )(
        cloud_x, cloud_y, mass_x.reshape(tiles, 128), mass_y.reshape(tiles, 128),
        left_start, right_start, jnp.tile(weight_start, 4)[None],
    )
    z = lax.axis_index("rank")
    start = (lax.rem(z, 4) * 128 + lax.div(z, 4) * 64,)
    return left, right, lax.dynamic_slice(weights.reshape(512), start, (ranks,))


def solution(mesh):
    in_specs = (
        P(None, "dp"),
        P(None, "dp"),
        P("dp"),
        P("dp"),
        P("rank", "dp"),
        P("rank", "dp"),
        P("rank"),
    )
    out_specs = (P("rank", "dp"), P("rank", "dp"), P("rank"))
    return jax.shard_map(shards, mesh=mesh, in_specs=in_specs, out_specs=out_specs, check_vma=False)
```

time: 244 us -> 209 us (0.86)
  Pallas kernels: 238 us -> 204 us
    pallas_call x1, Pallas kernels: 238 us -> 204 us  [shards(): pl.pallas_call(functools.partial(kernel, total_count), name='sinkhorn', o...]
where the time goes in v2:
time: 209 us
  Pallas kernels  204 us (98%)
  local copies, waits for them, and re-layouts  4.92 us (2%)
    pallas_call x1, Pallas kernels, shards(): pl.pallas_call(functools.partial(kernel, total_count), name='sinkhorn', o...  204 us

profile of v2, /device:TPU:1, one launch (start us, length us, event | category | flops | bytes accessed | tf_op | source)
XLA Modules:
  0.0 209.1 jit_solution(16194969627235811930)
XLA Ops:
  0.6 0.0 copy-start.1
  0.7 0.6 copy-done.1
  1.3 0.6 broadcast_in_dim_tile.3.w_ref
  1.9 203.5 %sinkhorn.1 = (f32[32,2048]{1,0:T(8,128)}, f32[32,2048]{1,0:T(8,128)}, f32[4,128]{1,0:T(4,128)}) custom-call(f32[64,2048]{1,0:T(8,128)} %x_ref.1, f32[64,2048]{1,0:T(8,128)} %y_ref.1, f32[16,128]{1,0:T(8,128)} %bitcast.3, f32[16,128]{1,0:T(8,128)} %bitcast.4, f32[32,2048]{1,0:T(8,128)} %left_ref.1, f32[32,2048]{1,0:T(8,128)} %right_ref.1, ...), custom_call_target="tpu_custom_call" | custom-call | tf_op jit(solution)/shard_map/sinkhorn/pallas_call | solution.py:423
  205.4 1.3 dynamic_slice.3
  206.7 0.0 copy-start
  206.7 1.7 copy.12
  208.4 0.0 copy-done
  208.4 0.7 copy.13
  (1 shorter events, 0.0 us)
Async XLA Ops:
  0.6 0.7 copy-start.1
  206.7 1.7 copy-start

commit v3 on v2

v3 whole, which is shorter than its diff:
```python
import functools

import jax
import jax.numpy as jnp
from jax import lax
from jax.experimental import pallas as pl
from jax.experimental.pallas import tpu as pltpu
from jax.sharding import PartitionSpec as P

RANK = 256
INNER = 4
MIRROR = 3
STEP = 2.0
MESH = pl.DeviceIdType.MESH
LOG2E = 1.4426950408889634

NX, NY, NC, NZ = 4, 8, 2, 8
NDP = NX * NY * NC


def far_first(n):
    return sorted(range(n), key=lambda d: -min(d, n - d))


DP_OFFSETS = sorted(
    [(dx, dy, dc) for dx in range(NX) for dy in range(NY) for dc in range(NC) if (dx, dy, dc) != (0, 0, 0)],
    key=lambda o: -(min(o[0], NX - o[0]) + min(o[1], NY - o[1])),
)
X_OFFSETS = [o for o in DP_OFFSETS if o[1] == 0 and o[2] == 0]
Y_OFFSETS = [o for o in DP_OFFSETS if o[0] == 0 and o[2] == 0]
Z_OFFSETS = [d for d in far_first(NZ) if d]


def cube_root(x):
    y = jnp.exp2(jnp.log2(x) * (1.0 / 3.0))
    y = y - (y - x / (y * y)) * (1.0 / 3.0)
    return jnp.where(x > 0.0, y, 0.0)


def split(x):
    high = x.astype(jnp.bfloat16)
    return high, (x - high.astype(jnp.float32)).astype(jnp.bfloat16)


def kernel(
    total_count,
    x_ref, y_ref, mx_ref, my_ref, left_ref, right_ref, w_ref,
    lo_ref, ro_ref, wo_ref,
    f_s, cl_s, m_s, k_s, cm_s, x4_s, w4_s, a_s, a1_s, n2_s, u_s, u1_s, uk_s, c_s, vb1_s, vb_s, fb_s, sb_s, o_s,
    v1_s, k1_s, sc_s, v_s, k3_s, g_s, veff_s, qs_s,
    zbuf, cbuf, dbuf, xbuf, ybuf, mbuf,
    zsend, zrecv, csend, crecv, dsend, drecv, xsend, xrecv, ysend, yrecv, msend, mrecv, asend, arecv, psend, precv,
):
    dp = lax.axis_index("dp")
    z = lax.axis_index("rank")
    core = lax.rem(dp, NC)
    twin = 1 - core
    yy = lax.rem(lax.div(dp, NC), NY)
    xx = lax.div(dp, NC * NY)
    chip = lax.div(dp, NC)
    tiles = left_ref.shape[1] // 128
    f32 = jnp.float32

    def dp_target(o):
        tx = lax.rem(xx + o[0], NX)
        ty = lax.rem(yy + o[1], NY)
        tc = lax.rem(core + o[2], NC)
        return ((tx * NY + ty) * NC + tc, z)

    def z_target(d):
        return (dp, lax.rem(z + d, NZ))

    def zc_target(d):
        return (chip * NC + twin, lax.rem(z + d, NZ))

    partner = (chip * NC + twin, z)
    z_targets = [z_target(d) for d in Z_OFFSETS]
    zc_targets = [t(d) for d in Z_OFFSETS for t in (zc_target, z_target)] + [partner]

    barrier = pltpu.get_barrier_semaphore()
    for d in Z_OFFSETS:
        pl.semaphore_signal(barrier, inc=1, device_id=z_target(d), device_id_type=MESH)
        pl.semaphore_signal(barrier, inc=1, device_id=zc_target(d), device_id_type=MESH)
    for o in DP_OFFSETS:
        pl.semaphore_signal(barrier, inc=1, device_id=dp_target(o), device_id_type=MESH)

    def send(slot, targets, ssem, rsem):
        for t in targets:
            pltpu.make_async_remote_copy(
                src_ref=slot, dst_ref=slot, send_sem=ssem, recv_sem=rsem, device_id=t, device_id_type=MESH
            ).start()

    def wait(some, ssem, rsem):
        pltpu.make_async_copy(some, some, rsem).wait()
        pltpu.make_async_copy(some, some, ssem).wait()

    def pair(i):
        src, dst = (
            (f_s.at[twin], k_s.at[z, core]),
            (m_s.at[twin], a_s.at[core]),
            (cl_s.at[twin], cm_s.at[core]),
            (u1_s.at[twin], u_s.at[core]),
            (o_s.at[0], o_s.at[1]),
        )[i]
        return pltpu.make_async_remote_copy(
            src_ref=src, dst_ref=dst, send_sem=psend.at[i], recv_sem=precv.at[i], device_id=partner, device_id_type=MESH
        )

    def end_pair(i):
        pair(i).wait_recv()
        pair(i).wait_send()

    def tile(t):
        return slice(t * 128, (t + 1) * 128)

    f_s[0] = left_ref[...]
    f_s[1] = right_ref[...]
    cl_s[0] = x_ref[...]
    cl_s[1] = y_ref[...]
    m_s[0] = mx_ref[...]
    m_s[1] = my_ref[...]
    a1_s[0:tiles, :] = mx_ref[...]
    a1_s[tiles:2 * tiles, :] = my_ref[...]
    lane = lax.broadcasted_iota(jnp.int32, (1, 128), 1)
    pl.semaphore_wait(barrier, 2 * len(Z_OFFSETS) + len(DP_OFFSETS))
    for i in range(3):
        pair(i).start()
    k_s[z, core] = f_s[core]
    a_s[core] = m_s[core]
    cm_s[core] = cl_s[core]

    def spread(vec):
        return jnp.broadcast_to(vec, (128, 128)).T

    def spread_all(dst, vec):
        for h in range(2):
            dst[h] = spread(vec[h:h + 1]).reshape(NZ, 16, 128)

    def gather_rows(rows):
        return jnp.sum(rows.T, axis=0, keepdims=True)

    def swap(p):
        return jnp.where(lax.rem(lane, 64) < 32, pltpu.roll(p, 96, 1), pltpu.roll(p, 32, 1))

    def doubled(c):
        return jnp.where(lane < 64, c, pltpu.roll(c, 64, 1))

    def ring_copies(i):
        hop, late = divmod(i, 2)
        copies = []
        for way, sign in ((0, 1), (1, -1)):
            part = k_s.at[lax.rem(z - sign * hop + NZ, NZ), (way + late) % 2]
            copies.append(pltpu.make_async_remote_copy(
                src_ref=part, dst_ref=part, send_sem=asend.at[i, way], recv_sem=arecv.at[i, way],
                device_id=(dp, lax.rem(z + sign + NZ, NZ)), device_id_type=MESH,
            ))
        return copies

    def ring_end(i):
        for copy in ring_copies(i):
            copy.wait_recv()
            copy.wait_send()

    def ring(i):
        if i >= 2:
            ring_end(i - 2)
        for copy in ring_copies(i):
            copy.start()

    def at(step, when, action):
        @pl.when(step == when)
        def _():
            action()

    def row_sums(step):
        par = lax.rem(step, 2)
        for t in range(tiles):
            for side in range(2):
                i = side * tiles + t
                b = f_s[side, :, tile(t)] * vb1_s[32 * side:32 * side + 32]
                zbuf[par, z, i:i + 1, :] = jnp.sum(b, axis=0, keepdims=True)
        send(zbuf.at[par, z], z_targets, zsend.at[par], zrecv.at[par])

        def first():
            end_pair(0)
            ring(0)
            end_pair(1)
            end_pair(2)
            prepare()

        at(step, 0, first)
        at(step, 2, lambda: ring(3))
        at(step, 3, lambda: ring(5))
        wait(zbuf.at[par, 0:NZ - 1], zsend.at[par], zrecv.at[par])
        total = zbuf[par, 0]
        for i in range(1, NZ):
            total = total + zbuf[par, i]
        u = a1_s[...] / total
        u1_s[0] = u[0:tiles]
        u1_s[1] = u[tiles:2 * tiles]

    def prepare():
        for s in range(2):
            for t in range(tiles):
                b = cm_s[s, :, tile(t)]
                n2_s[s, t:t + 1, :] = jnp.sum(b * b, axis=0, keepdims=True)
                high, low = split(b)
                both = jnp.concatenate([high, low], axis=0)
                x4_s[s, 0:128, tile(t)] = both
                x4_s[s, 128:256, tile(t)] = both

    def own_columns():
        accs = []
        for side in range(2):
            acc = jnp.zeros((32, 128), f32)
            for t in range(tiles):
                acc = acc + f_s[side, :, tile(t)] * jnp.broadcast_to(u1_s[side, t:t + 1, :], (32, 128))
            accs.append(acc)
        return accs

    def summed(buf, par, first, count):
        parts = [buf[par, first + i] for i in range(4)]
        for i in range(4, count):
            parts[i % 4] = parts[i % 4] + buf[par, first + i]
        return (parts[0] + parts[1]) + (parts[2] + parts[3])

    def exchange_first(par, low, high):
        cbuf[par, dp] = gather_rows(jnp.concatenate(low + high, axis=0))
        send(cbuf.at[par, dp], [dp_target(o) for o in DP_OFFSETS], csend.at[par], crecv.at[par])

    def rescale_first(c):
        v = v1_s[...]
        p = v * c
        g = cube_root(k1_s[...] * (p * swap(p)))
        v = g / c
        v1_s[...] = v
        return g, v

    def first_step(step, carry):
        par = lax.rem(step, 2)
        row_sums(step)
        ax = jnp.sum(a1_s[0:tiles, :], axis=0, keepdims=True)
        ay = jnp.sum(a1_s[tiles:2 * tiles, :], axis=0, keepdims=True)
        exchange_first(par, own_columns(), [jnp.broadcast_to(ax, (32, 128)), jnp.broadcast_to(ay, (32, 128))])
        at(step, 0, lambda: ring(1))
        at(step, 1, lambda: ring(2))
        at(step, 2, lambda: ring(4))
        wait(cbuf.at[par, 0:NDP - 1], csend.at[par], crecv.at[par])
        c = summed(cbuf, par, 0, NDP)
        scale = total_count / jnp.where(lane >= 64, c, pltpu.roll(c, 64, 1))
        sc_s[...] = scale
        g, v = rescale_first(doubled(c) * scale)
        vb1_s[...] = spread(v)[0:64]
        return carry

    def placed(row, offset):
        moved = pltpu.roll(jnp.broadcast_to(row, (8, 128)), lax.rem(z * 16 - offset + 256, 128), 1)[0:1]
        return jnp.where((lane >= z * 16) & (lane < z * 16 + 16), moved, 0.0)

    def start_moments():
        acc = jnp.zeros((32, 128), f32)
        both = jnp.zeros((32, 128), f32)
        for s in range(2):
            for t in range(tiles):
                b = k_s[z, s, :, tile(t)] * jnp.broadcast_to(u_s[s, t:t + 1, :], (32, 128))
                acc = acc + b * jnp.broadcast_to(n2_s[s, t:t + 1, :], (32, 128))
                high, low = split(b)
                uk_s[0:32, tile(t)] = high
                uk_s[32:64, tile(t)] = low
            d = lax.dot_general(
                uk_s[...], x4_s[s, 0:128, :], (((1,), (1,)), ((), ())), preferred_element_type=f32
            )
            both = both + d[0:32] + d[32:64]
        both = both + pltpu.roll(both, 64, 1)
        xbuf[xx, 0:16] = jnp.where(lane < 64, both[0:16], both[16:32])
        sums = gather_rows(jnp.concatenate([acc] * 4, axis=0))
        xbuf[xx, 16:17] = placed(sums, 0)
        xbuf[xx, 17:18] = placed(sums, 16)
        xbuf[xx, 18:24] = jnp.zeros((6, 128), f32)
        send(xbuf.at[xx], [dp_target(o) for o in X_OFFSETS], xsend, xrecv)

    def middle_moments():
        wait(xbuf.at[0:NX - 1], xsend, xrecv)
        m = xbuf[0]
        for i in range(1, NX):
            m = m + xbuf[i]
        ybuf[yy] = m
        send(ybuf.at[yy], [dp_target(o) for o in Y_OFFSETS], ysend, yrecv)

    def end_moments(par, rows):
        wait(ybuf.at[0:NY - 1], ysend, yrecv)
        m = ybuf[0]
        for i in range(1, NY):
            m = m + ybuf[i]
        slot = mbuf.at[par, core * NZ + z]
        slot[...] = m
        for i, row in enumerate(rows):
            slot[18 + i:19 + i] = row
        send(slot, zc_targets, msend.at[par], mrecv.at[par])

    v1_s[...] = jnp.ones((1, 128), f32)
    k1_s[...] = w_ref[...]
    vb1_s[...] = jnp.ones((64, 128), f32)
    lax.fori_loop(0, INNER - 1, first_step, 0)
    par = (INNER - 1) % 2
    row_sums(jnp.int32(INNER - 1))
    pair(3).start()
    u_s[core] = u1_s[core]
    accs = own_columns()
    exchange_first(par, accs, accs)
    end_pair(3)
    start_moments()
    ring(6)
    middle_moments()
    wait(cbuf.at[par, 0:NDP - 1], csend.at[par], crecv.at[par])
    c1 = summed(cbuf, par, 0, NDP) * sc_s[...]
    g1, v1 = rescale_first(c1)
    mine = core * 32
    e1 = v1 * sc_s[...]
    q1 = c1 * v1
    end_moments(0, [placed(p, mine + 16 * h) for p in (g1, e1, q1) for h in range(2)])
    ring_end(5)
    ring_end(6)
    wait(mbuf.at[0, 0:2 * NZ - 1], msend.at[0], mrecv.at[0])

    def over_blocks(par, cloud, first):
        rows = mbuf[par, cloud * NZ, first:first + 2]
        for b in range(1, NZ):
            rows = rows + mbuf[par, cloud * NZ + b, first:first + 2]
        return rows

    g_s[...] = over_blocks(0, core, 18)
    for i, cloud in enumerate((core, twin)):
        veff_s[i] = over_blocks(0, cloud, 20)
        qs_s[i] = over_blocks(0, cloud, 22)
    scales = [jnp.where(core == c, sc_s[...], pltpu.roll(sc_s[...], 32, 1)) for c in (0, 1)]
    for i in range(2):
        first = jnp.sum(jnp.where(lane == 0, scales[i], 0.0), axis=1, keepdims=True)
        a1_s[i:i + 1, :] = jnp.broadcast_to(first, (1, 128))

    def u_of_rows():
        for s in range(2):
            def body(b, accs):
                accs = list(accs)
                for j in range(4):
                    v = vb_s[j // 2, b, 8 * (j % 2):8 * (j % 2) + 8]
                    for t in range(tiles):
                        accs[t] = accs[t] + k_s[b, s, 8 * j:8 * j + 8, tile(t)] * v
                return tuple(accs)

            accs = lax.fori_loop(0, NZ, body, tuple(jnp.zeros((8, 128), f32) for _ in range(tiles)))
            for t in range(tiles):
                u_s[s, t:t + 1, :] = a_s[s, t:t + 1, :] / jnp.sum(accs[t], axis=0, keepdims=True)

    def start_columns(par):
        us = [[jnp.broadcast_to(u_s[s, t:t + 1, :], (8, 128)) for t in range(tiles)] for s in range(2)]

        def body(b, carry):
            for j in range(4):
                acc = [k_s[b, s, 8 * j:8 * j + 8, tile(t)] * us[s][t] for s in range(2) for t in range(tiles)]
                while len(acc) > 1:
                    acc = [p + q for p, q in zip(acc[::2], acc[1::2])]
                c_s[j // 2, b, 8 * (j % 2):8 * (j % 2) + 8] = acc[0]
            return carry

        lax.fori_loop(0, NZ, body, 0)
        slot = dbuf.at[par, core * (NDP // 2) + chip]
        slot[...] = jnp.concatenate([gather_rows(c_s[h].reshape(128, 128)) for h in range(2)], axis=0)
        send(slot, [dp_target(o) for o in DP_OFFSETS], dsend.at[par], drecv.at[par])

    def end_columns(par):
        wait(dbuf.at[par, 0:NDP - 1], dsend.at[par], drecv.at[par])
        c = [summed(dbuf, par, cloud * (NDP // 2), NDP // 2) * a1_s[i:i + 1] for i, cloud in enumerate((core, twin))]
        g = cube_root(k3_s[...] * ((v_s[0] * c[0]) * (v_s[1] * c[1])))
        for i in range(2):
            v_s[i] = g / c[i]
        return c, g

    def plain_step(step):
        par = lax.rem(step, 2)
        u_of_rows()
        start_columns(par)
        end_columns(par)
        spread_all(vb_s, v_s[0])

    def mirror(outer, carry):
        mpar = lax.rem(outer, 2)
        g = g_s[...]
        sq = [over_blocks(mpar, cloud, 16) * veff_s[i] for i, cloud in enumerate((core, twin))]
        cross = sq[0] * qs_s[1] + sq[1] * qs_s[0]
        prod = jnp.concatenate([mbuf[mpar, b, 0:16] * mbuf[mpar, NZ + b, 0:16] for b in range(NZ)], axis=0).T
        dots = jnp.concatenate([jnp.sum(prod[64 * h:64 * h + 64], axis=0, keepdims=True) for h in range(2)], axis=0)
        gg = -(cross - 2.0 * dots * (veff_s[0] * veff_s[1])) / (g * g)
        hh = sq[1] / g

        def mean(p):
            return jnp.sum(jnp.sum(p, axis=1, keepdims=True), axis=0, keepdims=True) / RANK

        k3_s[...] = g * jnp.exp(-STEP * (gg - mean(gg)))
        spread_all(fb_s, veff_s[1] * (2.0 * STEP * LOG2E) / g)
        spread_all(sb_s, (hh - mean(hh)) * (-STEP * LOG2E))
        spread_all(vb_s, veff_s[0])
        for b in range(NZ):
            m = mbuf[mpar, twin * NZ + b, 0:16]
            turned = pltpu.roll(m, 64, 1)
            for h, pair_of in ((0, jnp.where(lane < 64, m, turned)), (1, jnp.where(lane < 64, turned, m))):
                high, low = split(pair_of * fb_s[h, b])
                w4_s[32 * b + 16 * h:32 * b + 16 * h + 16, 0:128] = high
                w4_s[32 * b + 16 * h:32 * b + 16 * h + 16, 128:256] = low
        for s in range(2):
            for t in range(tiles // 2):
                cols = slice(t * 256, (t + 1) * 256)
                f = jnp.dot(w4_s[...], x4_s[s, :, cols], preferred_element_type=f32)
                ua = jnp.concatenate(
                    [jnp.broadcast_to(u_s[s, 2 * t + i:2 * t + i + 1, :], (16, 128)) for i in range(2)], axis=1
                )
                for b in range(NZ):
                    for h in range(2):
                        rows = slice(16 * h, 16 * h + 16)
                        sh = sb_s[h, b]
                        q = vb_s[h, b]
                        e = jnp.exp2(f[32 * b + 16 * h:32 * b + 16 * h + 16] + jnp.concatenate([sh, sh], axis=1))
                        k_s[b, s, rows, cols] = k_s[b, s, rows, cols] * ua * jnp.concatenate([q, q], axis=1) * e

        v_s[...] = jnp.ones((2, 2, 128), f32)
        vb_s[...] = jnp.ones((2, NZ, 16, 128), f32)
        base = outer * INNER

        def body(t, inner):
            plain_step(base + t)
            return inner

        lax.fori_loop(0, INNER - 1, body, 0)
        par = lax.rem(base + (INNER - 1), 2)
        npar = lax.rem(outer + 1, 2)
        u_of_rows()

        @pl.when(outer < MIRROR - 1)
        def _():
            start_moments()

        start_columns(par)

        @pl.when(outer < MIRROR - 1)
        def _():
            middle_moments()

        c, g = end_columns(par)
        g_s[...] = g
        for i in range(2):
            veff_s[i] = v_s[i] * a1_s[i:i + 1]
            qs_s[i] = c[i] * v_s[i]

        @pl.when(outer < MIRROR - 1)
        def _():
            end_moments(npar, ())
            wait(mbuf.at[npar, 0:2 * NZ - 1], msend.at[npar], mrecv.at[npar])

        return carry

    lax.fori_loop(0, MIRROR, mirror, 0)
    spread_all(vb_s, veff_s[0] * RANK)

    def result(s, t):
        q = jnp.concatenate([vb_s[0, z], vb_s[1, z]], axis=0)
        return k_s[z, s, :, tile(t)] * q * jnp.broadcast_to(u_s[s, t:t + 1, :], (32, 128))

    for t in range(tiles):
        o_s[0, :, tile(t)] = result(twin, t)
    pair(4).start()
    wo_ref[...] = g_s[...] * (RANK / total_count)
    for side, first, second in ((0, lo_ref, ro_ref), (1, ro_ref, lo_ref)):
        @pl.when(core == side)
        def _():
            for t in range(tiles):
                first[:, tile(t)] = result(core, t)
            end_pair(4)
            second[...] = o_s[1]


def shards(cloud_x, cloud_y, mass_x, mass_y, left_start, right_start, weight_start):
    ranks, points = left_start.shape
    total_count = float(points * lax.axis_size("dp"))
    tiles = points // 128
    f32 = jnp.float32
    bf16 = jnp.bfloat16
    dma = pltpu.SemaphoreType.DMA
    left, right, weights = pl.pallas_call(
        functools.partial(kernel, total_count),
        name="sinkhorn",
        out_shape=(
            jax.ShapeDtypeStruct((ranks, points), f32),
            jax.ShapeDtypeStruct((ranks, points), f32),
            jax.ShapeDtypeStruct((2, 128), f32),
        ),
        in_specs=[pl.BlockSpec(memory_space=pltpu.VMEM)] * 7,
        out_specs=[pl.BlockSpec(memory_space=pltpu.VMEM)] * 3,
        scratch_shapes=[
            pltpu.VMEM((2, ranks, points), f32),
            pltpu.VMEM((2, 64, points), f32),
            pltpu.VMEM((2, tiles, 128), f32),
            pltpu.VMEM((NZ, 2, ranks, points), f32),
            pltpu.VMEM((2, 64, points), f32),
            pltpu.VMEM((2, 256, points), bf16),
            pltpu.VMEM((256, 256), bf16),
            pltpu.VMEM((2, tiles, 128), f32),
            pltpu.VMEM((2 * tiles, 128), f32),
            pltpu.VMEM((2, tiles, 128), f32),
            pltpu.VMEM((2, tiles, 128), f32),
            pltpu.VMEM((2, tiles, 128), f32),
            pltpu.VMEM((64, points), bf16),
            pltpu.VMEM((2, NZ, 16, 128), f32),
            pltpu.VMEM((64, 128), f32),
            pltpu.VMEM((2, NZ, 16, 128), f32),
            pltpu.VMEM((2, NZ, 16, 128), f32),
            pltpu.VMEM((2, NZ, 16, 128), f32),
            pltpu.VMEM((2, ranks, points), f32),
            pltpu.VMEM((1, 128), f32),
            pltpu.VMEM((1, 128), f32),
            pltpu.VMEM((1, 128), f32),
            pltpu.VMEM((2, 2, 128), f32),
            pltpu.VMEM((2, 128), f32),
            pltpu.VMEM((2, 128), f32),
            pltpu.VMEM((2, 2, 128), f32),
            pltpu.VMEM((2, 2, 128), f32),
            pltpu.VMEM((2, NZ, 2 * tiles, 128), f32),
            pltpu.VMEM((2, NDP, 1, 128), f32),
            pltpu.VMEM((2, NDP, 2, 128), f32),
            pltpu.VMEM((NX, 24, 128), f32),
            pltpu.VMEM((NY, 24, 128), f32),
            pltpu.VMEM((2, 2 * NZ, 24, 128), f32),
            dma((2,)), dma((2,)), dma((2,)), dma((2,)), dma((2,)), dma((2,)),
            dma, dma, dma, dma, dma((2,)), dma((2,)),
            dma((NZ - 1, 2)), dma((NZ - 1, 2)), dma((5,)), dma((5,)),
        ],
        compiler_params=pltpu.CompilerParams(collective_id=0, has_side_effects=True),
    )(
        cloud_x, cloud_y, mass_x.reshape(tiles, 128), mass_y.reshape(tiles, 128),
        left_start, right_start, jnp.tile(weight_start, 4)[None],
    )
    z = lax.axis_index("rank")
    own = lax.dynamic_slice(weights.reshape(2, NZ, 16), (0, z, 0), (2, 1, 16))
    return left, right, own.reshape(ranks)


def solution(mesh):
    in_specs = (
        P(None, "dp"),
        P(None, "dp"),
        P("dp"),
        P("dp"),
        P("rank", "dp"),
        P("rank", "dp"),
        P("rank"),
    )
    out_specs = (P("rank", "dp"), P("rank", "dp"), P("rank"))
    return jax.shard_map(shards, mesh=mesh, in_specs=in_specs, out_specs=out_specs, check_vma=False)
```

time: 209 us -> 189 us (0.904)
  Pallas kernels: 204 us -> 183 us
    pallas_call x1, Pallas kernels: 204 us -> 183 us  [shards(): pl.pallas_call(functools.partial(kernel, total_count), name='sinkhorn', o...]
where the time goes in v3:
time: 189 us
  Pallas kernels  183 us (97%)
  local copies, waits for them, and re-layouts  5.01 us (3%)
    pallas_call x1, Pallas kernels, shards(): pl.pallas_call(functools.partial(kernel, total_count), name='sinkhorn', o...  183 us

profile of v3, /device:TPU:1, one launch (start us, length us, event | category | flops | bytes accessed | tf_op | source)
XLA Modules:
  0.0 189.1 jit_solution(11686812916673719889)
XLA Ops:
  0.6 0.0 copy-start.2
  0.6 0.6 copy-done.2
  1.3 0.6 broadcast_in_dim_tile.3.w_ref
  1.9 183.5 %sinkhorn.1 = (f32[32,2048]{1,0:T(8,128)}, f32[32,2048]{1,0:T(8,128)}, f32[2,128]{1,0:T(2,128)}) custom-call(f32[64,2048]{1,0:T(8,128)} %x_ref.1, f32[64,2048]{1,0:T(8,128)} %y_ref.1, f32[16,128]{1,0:T(8,128)} %bitcast.5, f32[16,128]{1,0:T(8,128)} %bitcast.6, f32[32,2048]{1,0:T(8,128)} %left_ref.1, f32[32,2048]{1,0:T(8,128)} %right_ref.1, ...), custom_call_target="tpu_custom_call" | custom-call | tf_op jit(solution)/shard_map/sinkhorn/pallas_call | solution.py:488
  185.4 0.0 copy-start.1
  185.4 0.7 copy-done.1
  186.0 0.1 reshape.21
  186.1 0.6 reshape.22
  186.7 0.0 copy-start
  186.7 1.7 copy.14
  188.4 0.0 copy-done
  188.4 0.7 copy.15
  (2 shorter events, 0.0 us)
Async XLA Ops:
  0.6 0.7 copy-start.2
  185.4 0.7 copy-start.1
  186.7 1.7 copy-start

commit v4 on v3

--- a/solution.py
+++ b/solution.py
@@ -45,11 +45,11 @@
 def kernel(
     total_count,
     x_ref, y_ref, mx_ref, my_ref, left_ref, right_ref, w_ref,
-    lo_ref, ro_ref, wo_ref,
-    f_s, cl_s, m_s, k_s, cm_s, x4_s, w4_s, a_s, a1_s, n2_s, u_s, u1_s, uk_s, c_s, vb1_s, vb_s, fb_s, sb_s, o_s,
+    ku_ref, vo_ref, wo_ref,
+    w_s, f_s, cl_s, m_s, k_s, cm_s, x4_s, w4_s, a_s, a1_s, n2_s, u_s, u1_s, uk_s, c_s, vb1_s, vb_s, fb_s, sb_s, o_s, ou_s, ku_s,
     v1_s, k1_s, sc_s, v_s, k3_s, g_s, veff_s, qs_s,
     zbuf, cbuf, dbuf, xbuf, ybuf, mbuf,
-    zsend, zrecv, csend, crecv, dsend, drecv, xsend, xrecv, ysend, yrecv, msend, mrecv, asend, arecv, psend, precv,
+    zsend, zrecv, csend, crecv, dsend, drecv, xsend, xrecv, ysend, yrecv, msend, mrecv, asend, arecv, psend, precv, isem,
 ):
     dp = lax.axis_index("dp")
     z = lax.axis_index("rank")
@@ -58,7 +58,7 @@
     yy = lax.rem(lax.div(dp, NC), NY)
     xx = lax.div(dp, NC * NY)
     chip = lax.div(dp, NC)
-    tiles = left_ref.shape[1] // 128
+    tiles = mx_ref.shape[0]
     f32 = jnp.float32
 
     def dp_target(o):
@@ -100,12 +100,16 @@
             (m_s.at[twin], a_s.at[core]),
             (cl_s.at[twin], cm_s.at[core]),
             (u1_s.at[twin], u_s.at[core]),
-            (o_s.at[0], o_s.at[1]),
+            (k_s.at[z, twin], o_s),
+            (u_s.at[twin], ou_s),
         )[i]
         return pltpu.make_async_remote_copy(
             src_ref=src, dst_ref=dst, send_sem=psend.at[i], recv_sem=precv.at[i], device_id=partner, device_id_type=MESH
         )
 
+    def scaled():
+        return pltpu.make_async_copy(ku_s, ku_ref, isem.at[7])
+
     def end_pair(i):
         pair(i).wait_recv()
         pair(i).wait_send()
@@ -113,21 +117,30 @@
     def tile(t):
         return slice(t * 128, (t + 1) * 128)
 
-    f_s[0] = left_ref[...]
-    f_s[1] = right_ref[...]
-    cl_s[0] = x_ref[...]
-    cl_s[1] = y_ref[...]
-    m_s[0] = mx_ref[...]
-    m_s[1] = my_ref[...]
-    a1_s[0:tiles, :] = mx_ref[...]
-    a1_s[tiles:2 * tiles, :] = my_ref[...]
+    inputs = [
+        pltpu.make_async_copy(src, dst, isem.at[i])
+        for i, (src, dst) in enumerate((
+            (left_ref, f_s.at[0]), (right_ref, f_s.at[1]), (mx_ref, m_s.at[0]), (my_ref, m_s.at[1]),
+            (x_ref, cl_s.at[0]), (y_ref, cl_s.at[1]), (w_ref, w_s),
+        ))
+    ]
+    for copy in inputs:
+        copy.start()
     lane = lax.broadcasted_iota(jnp.int32, (1, 128), 1)
+    for copy in inputs:
+        copy.wait()
+    a1_s[0:tiles, :] = m_s[0]
+    a1_s[tiles:2 * tiles, :] = m_s[1]
+    k_s[z, core] = f_s[core]
+    a_s[core] = m_s[core]
+    cm_s[core] = cl_s[core]
+    k1_s[0:1, 0:w_s.shape[1]] = w_s[...]
+    start = jnp.where(lane < 32, k1_s[...], 0.0)
+    start = start + pltpu.roll(start, 32, 1)
+    k1_s[...] = start + pltpu.roll(start, 64, 1)
     pl.semaphore_wait(barrier, 2 * len(Z_OFFSETS) + len(DP_OFFSETS))
     for i in range(3):
         pair(i).start()
-    k_s[z, core] = f_s[core]
-    a_s[core] = m_s[core]
-    cm_s[core] = cl_s[core]
 
     def spread(vec):
         return jnp.broadcast_to(vec, (128, 128)).T
@@ -299,7 +312,6 @@
         send(slot, zc_targets, msend.at[par], mrecv.at[par])
 
     v1_s[...] = jnp.ones((1, 128), f32)
-    k1_s[...] = w_ref[...]
     vb1_s[...] = jnp.ones((64, 128), f32)
     lax.fori_loop(0, INNER - 1, first_step, 0)
     par = (INNER - 1) % 2
@@ -378,10 +390,10 @@
 
     def plain_step(step):
         par = lax.rem(step, 2)
-        u_of_rows()
         start_columns(par)
         end_columns(par)
         spread_all(vb_s, v_s[0])
+        u_of_rows()
 
     def mirror(outer, carry):
         mpar = lax.rem(outer, 2)
@@ -414,16 +426,27 @@
                 ua = jnp.concatenate(
                     [jnp.broadcast_to(u_s[s, 2 * t + i:2 * t + i + 1, :], (16, 128)) for i in range(2)], axis=1
                 )
+                acc = jnp.zeros((8, 256), f32)
                 for b in range(NZ):
                     for h in range(2):
                         rows = slice(16 * h, 16 * h + 16)
                         sh = sb_s[h, b]
                         q = vb_s[h, b]
                         e = jnp.exp2(f[32 * b + 16 * h:32 * b + 16 * h + 16] + jnp.concatenate([sh, sh], axis=1))
-                        k_s[b, s, rows, cols] = k_s[b, s, rows, cols] * ua * jnp.concatenate([q, q], axis=1) * e
+                        new = k_s[b, s, rows, cols] * ua * jnp.concatenate([q, q], axis=1) * e
+                        k_s[b, s, rows, cols] = new
+                        acc = acc + (new[0:8] + new[8:16])
+                total = jnp.sum(acc, axis=0, keepdims=True)
+                for i in range(2):
+                    r = 2 * t + i
+                    u_s[s, r:r + 1, :] = a_s[s, r:r + 1, :] / total[:, 128 * i:128 * i + 128]
 
         v_s[...] = jnp.ones((2, 2, 128), f32)
-        vb_s[...] = jnp.ones((2, NZ, 16, 128), f32)
+
+        @pl.when(outer == MIRROR - 1)
+        def _():
+            pair(4).start()
+
         base = outer * INNER
 
         def body(t, inner):
@@ -433,17 +456,30 @@
         lax.fori_loop(0, INNER - 1, body, 0)
         par = lax.rem(base + (INNER - 1), 2)
         npar = lax.rem(outer + 1, 2)
-        u_of_rows()
 
         @pl.when(outer < MIRROR - 1)
         def _():
             start_moments()
 
+        @pl.when(outer == MIRROR - 1)
+        def _():
+            pair(5).start()
+
         start_columns(par)
 
         @pl.when(outer < MIRROR - 1)
         def _():
             middle_moments()
+
+        @pl.when(outer == MIRROR - 1)
+        def _():
+            for t in range(tiles):
+                ku_s[core, :, tile(t)] = k_s[z, core, :, tile(t)] * jnp.broadcast_to(u_s[core, t:t + 1, :], (32, 128))
+            end_pair(4)
+            end_pair(5)
+            for t in range(tiles):
+                ku_s[twin, :, tile(t)] = o_s[:, tile(t)] * jnp.broadcast_to(ou_s[t:t + 1, :], (32, 128))
+            scaled().start()
 
         c, g = end_columns(par)
         g_s[...] = g
@@ -459,23 +495,23 @@
         return carry
 
     lax.fori_loop(0, MIRROR, mirror, 0)
-    spread_all(vb_s, veff_s[0] * RANK)
-
-    def result(s, t):
-        q = jnp.concatenate([vb_s[0, z], vb_s[1, z]], axis=0)
-        return k_s[z, s, :, tile(t)] * q * jnp.broadcast_to(u_s[s, t:t + 1, :], (32, 128))
-
-    for t in range(tiles):
-        o_s[0, :, tile(t)] = result(twin, t)
-    pair(4).start()
-    wo_ref[...] = g_s[...] * (RANK / total_count)
-    for side, first, second in ((0, lo_ref, ro_ref), (1, ro_ref, lo_ref)):
-        @pl.when(core == side)
-        def _():
-            for t in range(tiles):
-                first[:, tile(t)] = result(core, t)
-            end_pair(4)
-            second[...] = o_s[1]
+    for i, cloud in ((0, core), (1, twin)):
+        spread_all((vb_s, fb_s)[i], veff_s[i] * RANK)
+        for h in range(2):
+            vo_ref[cloud, 16 * h:16 * h + 16] = (vb_s, fb_s)[i][h, z]
+    own = [
+        pltpu.roll(jnp.broadcast_to(g_s[h:h + 1], (8, 128)), lax.rem(128 + 16 * h - z * 16, 128), 1)[0:1] for h in range(2)
+    ]
+    wo_ref[...] = jnp.where(lane < 16, own[0], own[1]) * (RANK / total_count)
+    scaled().wait()
+
+
+def finish(ku_ref, vo_ref, w_ref, lo_ref, ro_ref, wo_ref):
+    for side, ref in ((0, lo_ref), (1, ro_ref)):
+        for t in range(ref.shape[1] // 128):
+            cols = slice(t * 128, (t + 1) * 128)
+            ref[:, cols] = ku_ref[side, :, cols] * vo_ref[side]
+    wo_ref[...] = w_ref[:, 0:wo_ref.shape[1]]
 
 
 def shards(cloud_x, cloud_y, mass_x, mass_y, left_start, right_start, weight_start):
@@ -485,17 +521,19 @@
     f32 = jnp.float32
     bf16 = jnp.bfloat16
     dma = pltpu.SemaphoreType.DMA
-    left, right, weights = pl.pallas_call(
+    vmem = pl.BlockSpec(memory_space=pltpu.VMEM)
+    scaled, scales, weights = pl.pallas_call(
         functools.partial(kernel, total_count),
         name="sinkhorn",
         out_shape=(
-            jax.ShapeDtypeStruct((ranks, points), f32),
-            jax.ShapeDtypeStruct((ranks, points), f32),
-            jax.ShapeDtypeStruct((2, 128), f32),
+            jax.ShapeDtypeStruct((2, ranks, points), f32),
+            jax.ShapeDtypeStruct((2, ranks, 128), f32),
+            jax.ShapeDtypeStruct((1, 128), f32),
         ),
-        in_specs=[pl.BlockSpec(memory_space=pltpu.VMEM)] * 7,
-        out_specs=[pl.BlockSpec(memory_space=pltpu.VMEM)] * 3,
+        in_specs=[pl.BlockSpec(memory_space=pl.ANY)] * 7,
+        out_specs=[pl.BlockSpec(memory_space=pl.ANY), vmem, vmem],
         scratch_shapes=[
+            pltpu.VMEM((1, ranks), f32),
             pltpu.VMEM((2, ranks, points), f32),
             pltpu.VMEM((2, 64, points), f32),
             pltpu.VMEM((2, tiles, 128), f32),
@@ -514,6 +552,8 @@
             pltpu.VMEM((2, NZ, 16, 128), f32),
             pltpu.VMEM((2, NZ, 16, 128), f32),
             pltpu.VMEM((2, NZ, 16, 128), f32),
+            pltpu.VMEM((ranks, points), f32),
+            pltpu.VMEM((tiles, 128), f32),
             pltpu.VMEM((2, ranks, points), f32),
             pltpu.VMEM((1, 128), f32),
             pltpu.VMEM((1, 128), f32),
@@ -531,16 +571,25 @@
             pltpu.VMEM((2, 2 * NZ, 24, 128), f32),
             dma((2,)), dma((2,)), dma((2,)), dma((2,)), dma((2,)), dma((2,)),
             dma, dma, dma, dma, dma((2,)), dma((2,)),
-            dma((NZ - 1, 2)), dma((NZ - 1, 2)), dma((5,)), dma((5,)),
+            dma((NZ - 1, 2)), dma((NZ - 1, 2)), dma((6,)), dma((6,)), dma((8,)),
         ],
         compiler_params=pltpu.CompilerParams(collective_id=0, has_side_effects=True),
     )(
         cloud_x, cloud_y, mass_x.reshape(tiles, 128), mass_y.reshape(tiles, 128),
-        left_start, right_start, jnp.tile(weight_start, 4)[None],
+        left_start, right_start, weight_start[None],
     )
-    z = lax.axis_index("rank")
-    own = lax.dynamic_slice(weights.reshape(2, NZ, 16), (0, z, 0), (2, 1, 16))
-    return left, right, own.reshape(ranks)
+    left, right, weights = pl.pallas_call(
+        finish,
+        name="finish",
+        out_shape=(
+            jax.ShapeDtypeStruct((ranks, points), f32),
+            jax.ShapeDtypeStruct((ranks, points), f32),
+            jax.ShapeDtypeStruct((1, ranks), f32),
+        ),
+        in_specs=[vmem] * 3,
+        out_specs=[vmem] * 3,
+    )(scaled, scales, weights)
+    return left, right, weights.reshape(ranks)
 
 
 def solution(mesh):

time: 189 us -> 183 us (0.968)
  local copies, waits for them, and re-layouts: 5.01 us -> 0 us
    unnamed x8 -> x0, local copies, waits for them, and re-layouts: 3.73 us -> none
    pallas_call x1, Pallas kernels: 183 us -> 180 us  [shards(): pl.pallas_call(functools.partial(kernel, total_count), name='sinkhorn', o...]
where the time goes in v4:
time: 183 us
  Pallas kernels  182 us (99%)
    pallas_call x1, Pallas kernels, shards(): pl.pallas_call(functools.partial(kernel, total_count), name='sinkhorn', o...  180 us

profile of v4, /device:TPU:1, one launch (start us, length us, event | category | flops | bytes accessed | tf_op | source)
XLA Modules:
  0.0 182.5 jit_solution(2274803588315787627)
XLA Ops:
  0.6 180.0 %sinkhorn.1 = (f32[2,32,2048]{2,1,0:T(8,128)}, f32[2,32,128]{2,1,0:T(8,128)}, f32[1,128]{1,0:T(1,128)}) custom-call(f32[64,2048]{1,0:T(8,128)} %x_ref.1, f32[64,2048]{1,0:T(8,128)} %y_ref.1, f32[16,128]{1,0:T(8,128)} %bitcast.4, f32[16,128]{1,0:T(8,128)} %bitcast.5, f32[32,2048]{1,0:T(8,128)} %left_ref.1, f32[32,2048]{1,0:T(8,128)} %right_ref.1, f32[1,32]{1,0:T(1,128)} %bitcast.6), custom_call_target="tpu_custom_call" | custom-call | tf_op jit(solution)/shard_map/sinkhorn/pallas_call | solution.py:525
  180.6 1.9 %finish.1 = (f32[32,2048]{1,0:T(8,128)}, f32[32,2048]{1,0:T(8,128)}, f32[1,32]{1,0:T(1,128)}) custom-call(f32[2,32,2048]{2,1,0:T(8,128)} %get-tuple-element.9.ku_ref, f32[2,32,128]{2,1,0:T(8,128)} %get-tuple-element.10.vo_ref, f32[1,128]{1,0:T(1,128)} %get-tuple-element.11.w_ref), custom_call_target="tpu_custom_call" | custom-call | tf_op jit(solution)/shard_map/finish/pallas_call | solution.py:581

commit v5 on v4

--- a/solution.py
+++ b/solution.py
@@ -278,10 +278,10 @@
                 b = k_s[z, s, :, tile(t)] * jnp.broadcast_to(u_s[s, t:t + 1, :], (32, 128))
                 acc = acc + b * jnp.broadcast_to(n2_s[s, t:t + 1, :], (32, 128))
                 high, low = split(b)
-                uk_s[0:32, tile(t)] = high
-                uk_s[32:64, tile(t)] = low
+                uk_s[s, 0:32, tile(t)] = high
+                uk_s[s, 32:64, tile(t)] = low
             d = lax.dot_general(
-                uk_s[...], x4_s[s, 0:128, :], (((1,), (1,)), ((), ())), preferred_element_type=f32
+                uk_s[s], x4_s[s, 0:128, :], (((1,), (1,)), ((), ())), preferred_element_type=f32
             )
             both = both + d[0:32] + d[32:64]
         both = both + pltpu.roll(both, 64, 1)
@@ -289,7 +289,6 @@
         sums = gather_rows(jnp.concatenate([acc] * 4, axis=0))
         xbuf[xx, 16:17] = placed(sums, 0)
         xbuf[xx, 17:18] = placed(sums, 16)
-        xbuf[xx, 18:24] = jnp.zeros((6, 128), f32)
         send(xbuf.at[xx], [dp_target(o) for o in X_OFFSETS], xsend, xrecv)
 
     def middle_moments():
@@ -305,11 +304,10 @@
         m = ybuf[0]
         for i in range(1, NY):
             m = m + ybuf[i]
-        slot = mbuf.at[par, core * NZ + z]
-        slot[...] = m
+        mbuf[par, core * NZ + z, 0:18] = m
         for i, row in enumerate(rows):
-            slot[18 + i:19 + i] = row
-        send(slot, zc_targets, msend.at[par], mrecv.at[par])
+            mbuf[par, core * NZ + z, 18 + i:19 + i] = row
+        send(mbuf.at[par, core * NZ + z, 0:18 + len(rows)], zc_targets, msend.at[par], mrecv.at[par])
 
     v1_s[...] = jnp.ones((1, 128), f32)
     vb1_s[...] = jnp.ones((64, 128), f32)
@@ -360,7 +358,7 @@
                         accs[t] = accs[t] + k_s[b, s, 8 * j:8 * j + 8, tile(t)] * v
                 return tuple(accs)
 
-            accs = lax.fori_loop(0, NZ, body, tuple(jnp.zeros((8, 128), f32) for _ in range(tiles)))
+            accs = lax.fori_loop(0, NZ, body, tuple(jnp.zeros((8, 128), f32) for _ in range(tiles)), unroll=True)
             for t in range(tiles):
                 u_s[s, t:t + 1, :] = a_s[s, t:t + 1, :] / jnp.sum(accs[t], axis=0, keepdims=True)
 
@@ -375,7 +373,7 @@
                 c_s[j // 2, b, 8 * (j % 2):8 * (j % 2) + 8] = acc[0]
             return carry
 
-        lax.fori_loop(0, NZ, body, 0)
+        lax.fori_loop(0, NZ, body, 0, unroll=True)
         slot = dbuf.at[par, core * (NDP // 2) + chip]
         slot[...] = jnp.concatenate([gather_rows(c_s[h].reshape(128, 128)) for h in range(2)], axis=0)
         send(slot, [dp_target(o) for o in DP_OFFSETS], dsend.at[par], drecv.at[par])
@@ -490,7 +488,7 @@
         @pl.when(outer < MIRROR - 1)
         def _():
             end_moments(npar, ())
-            wait(mbuf.at[npar, 0:2 * NZ - 1], msend.at[npar], mrecv.at[npar])
+            wait(mbuf.at[npar, 0:2 * NZ - 1, 0:18], msend.at[npar], mrecv.at[npar])
 
         return carry
 
@@ -546,7 +544,7 @@
             pltpu.VMEM((2, tiles, 128), f32),
             pltpu.VMEM((2, tiles, 128), f32),
             pltpu.VMEM((2, tiles, 128), f32),
-            pltpu.VMEM((64, points), bf16),
+            pltpu.VMEM((2, 64, points), bf16),
             pltpu.VMEM((2, NZ, 16, 128), f32),
             pltpu.VMEM((64, 128), f32),
             pltpu.VMEM((2, NZ, 16, 128), f32),
@@ -566,8 +564,8 @@
             pltpu.VMEM((2, NZ, 2 * tiles, 128), f32),
             pltpu.VMEM((2, NDP, 1, 128), f32),
             pltpu.VMEM((2, NDP, 2, 128), f32),
-            pltpu.VMEM((NX, 24, 128), f32),
-            pltpu.VMEM((NY, 24, 128), f32),
+            pltpu.VMEM((NX, 18, 128), f32),
+            pltpu.VMEM((NY, 18, 128), f32),
             pltpu.VMEM((2, 2 * NZ, 24, 128), f32),
             dma((2,)), dma((2,)), dma((2,)), dma((2,)), dma((2,)), dma((2,)),
             dma, dma, dma, dma, dma((2,)), dma((2,)),

time: 183 us -> 179 us (0.978)
  Pallas kernels: 182 us -> 179 us
    pallas_call x1, Pallas kernels: 180 us -> 177 us  [shards(): pl.pallas_call(functools.partial(kernel, total_count), name='sinkhorn', o...]
where the time goes in v5:
time: 179 us
  Pallas kernels  179 us (100%)
    pallas_call x1, Pallas kernels, shards(): pl.pallas_call(functools.partial(kernel, total_count), name='sinkhorn', o...  177 us

profile of v5, /device:TPU:1, one launch (start us, length us, event | category | flops | bytes accessed | tf_op | source)
XLA Modules:
  0.0 179.2 jit_solution(9773255422537215784)
XLA Ops:
  0.6 176.7 %sinkhorn.1 = (f32[2,32,2048]{2,1,0:T(8,128)}, f32[2,32,128]{2,1,0:T(8,128)}, f32[1,128]{1,0:T(1,128)}) custom-call(f32[64,2048]{1,0:T(8,128)} %x_ref.1, f32[64,2048]{1,0:T(8,128)} %y_ref.1, f32[16,128]{1,0:T(8,128)} %bitcast.4, f32[16,128]{1,0:T(8,128)} %bitcast.5, f32[32,2048]{1,0:T(8,128)} %left_ref.1, f32[32,2048]{1,0:T(8,128)} %right_ref.1, f32[1,32]{1,0:T(1,128)} %bitcast.6), custom_call_target="tpu_custom_call" | custom-call | tf_op jit(solution)/shard_map/sinkhorn/pallas_call | solution.py:523
  177.3 1.9 %finish.1 = (f32[32,2048]{1,0:T(8,128)}, f32[32,2048]{1,0:T(8,128)}, f32[1,32]{1,0:T(1,128)}) custom-call(f32[2,32,2048]{2,1,0:T(8,128)} %get-tuple-element.9.ku_ref, f32[2,32,128]{2,1,0:T(8,128)} %get-tuple-element.10.vo_ref, f32[1,128]{1,0:T(1,128)} %get-tuple-element.11.w_ref), custom_call_target="tpu_custom_call" | custom-call | tf_op jit(solution)/shard_map/finish/pallas_call | solution.py:579

commit v6 on v5

--- a/solution.py
+++ b/solution.py
@@ -77,6 +77,15 @@
     z_targets = [z_target(d) for d in Z_OFFSETS]
     zc_targets = [t(d) for d in Z_OFFSETS for t in (zc_target, z_target)] + [partner]
 
+    inputs = [
+        pltpu.make_async_copy(src, dst, isem.at[i])
+        for i, (src, dst) in enumerate((
+            (left_ref, f_s.at[0]), (right_ref, f_s.at[1]), (mx_ref, m_s.at[0]), (my_ref, m_s.at[1]),
+            (x_ref, cl_s.at[0]), (y_ref, cl_s.at[1]), (w_ref, w_s),
+        ))
+    ]
+    for copy in inputs:
+        copy.start()
     barrier = pltpu.get_barrier_semaphore()
     for d in Z_OFFSETS:
         pl.semaphore_signal(barrier, inc=1, device_id=z_target(d), device_id_type=MESH)
@@ -117,15 +126,13 @@
     def tile(t):
         return slice(t * 128, (t + 1) * 128)
 
-    inputs = [
-        pltpu.make_async_copy(src, dst, isem.at[i])
-        for i, (src, dst) in enumerate((
-            (left_ref, f_s.at[0]), (right_ref, f_s.at[1]), (mx_ref, m_s.at[0]), (my_ref, m_s.at[1]),
-            (x_ref, cl_s.at[0]), (y_ref, cl_s.at[1]), (w_ref, w_s),
-        ))
-    ]
-    for copy in inputs:
-        copy.start()
+    def own_rows(par):
+        for t in range(tiles):
+            for side in range(2):
+                i = side * tiles + t
+                b = f_s[side, :, tile(t)] * vb1_s[32 * side:32 * side + 32]
+                zbuf[par, z, i:i + 1, :] = jnp.sum(b, axis=0, keepdims=True)
+
     lane = lax.broadcasted_iota(jnp.int32, (1, 128), 1)
     for copy in inputs:
         copy.wait()
@@ -138,6 +145,9 @@
     start = jnp.where(lane < 32, k1_s[...], 0.0)
     start = start + pltpu.roll(start, 32, 1)
     k1_s[...] = start + pltpu.roll(start, 64, 1)
+    v1_s[...] = jnp.ones((1, 128), f32)
+    vb1_s[...] = jnp.ones((64, 128), f32)
+    own_rows(0)
     pl.semaphore_wait(barrier, 2 * len(Z_OFFSETS) + len(DP_OFFSETS))
     for i in range(3):
         pair(i).start()
@@ -187,11 +197,6 @@
 
     def row_sums(step):
         par = lax.rem(step, 2)
-        for t in range(tiles):
-            for side in range(2):
-                i = side * tiles + t
-                b = f_s[side, :, tile(t)] * vb1_s[32 * side:32 * side + 32]
-                zbuf[par, z, i:i + 1, :] = jnp.sum(b, axis=0, keepdims=True)
         send(zbuf.at[par, z], z_targets, zsend.at[par], zrecv.at[par])
 
         def first():
@@ -264,24 +269,27 @@
         sc_s[...] = scale
         g, v = rescale_first(doubled(c) * scale)
         vb1_s[...] = spread(v)[0:64]
+        own_rows(1 - par)
         return carry
 
     def placed(row, offset):
         moved = pltpu.roll(jnp.broadcast_to(row, (8, 128)), lax.rem(z * 16 - offset + 256, 128), 1)[0:1]
         return jnp.where((lane >= z * 16) & (lane < z * 16 + 16), moved, 0.0)
 
-    def start_moments():
+    def start_moments(between=None):
         acc = jnp.zeros((32, 128), f32)
         both = jnp.zeros((32, 128), f32)
-        for s in range(2):
+        for i, s in enumerate((core, twin)):
+            if i and between:
+                between()
             for t in range(tiles):
                 b = k_s[z, s, :, tile(t)] * jnp.broadcast_to(u_s[s, t:t + 1, :], (32, 128))
                 acc = acc + b * jnp.broadcast_to(n2_s[s, t:t + 1, :], (32, 128))
                 high, low = split(b)
-                uk_s[s, 0:32, tile(t)] = high
-                uk_s[s, 32:64, tile(t)] = low
+                uk_s[i, 0:32, tile(t)] = high
+                uk_s[i, 32:64, tile(t)] = low
             d = lax.dot_general(
-                uk_s[s], x4_s[s, 0:128, :], (((1,), (1,)), ((), ())), preferred_element_type=f32
+                uk_s[i], x4_s[s, 0:128, :], (((1,), (1,)), ((), ())), preferred_element_type=f32
             )
             both = both + d[0:32] + d[32:64]
         both = both + pltpu.roll(both, 64, 1)
@@ -309,8 +317,6 @@
             mbuf[par, core * NZ + z, 18 + i:19 + i] = row
         send(mbuf.at[par, core * NZ + z, 0:18 + len(rows)], zc_targets, msend.at[par], mrecv.at[par])
 
-    v1_s[...] = jnp.ones((1, 128), f32)
-    vb1_s[...] = jnp.ones((64, 128), f32)
     lax.fori_loop(0, INNER - 1, first_step, 0)
     par = (INNER - 1) % 2
     row_sums(jnp.int32(INNER - 1))
@@ -318,8 +324,7 @@
     u_s[core] = u1_s[core]
     accs = own_columns()
     exchange_first(par, accs, accs)
-    end_pair(3)
-    start_moments()
+    start_moments(lambda: end_pair(3))
     ring(6)
     middle_moments()
     wait(cbuf.at[par, 0:NDP - 1], csend.at[par], crecv.at[par])

time: 179 us -> 179 us (level)
  no operation moved by 1% of the time
where the time goes in v6:
time: 179 us
  Pallas kernels  178 us (99%)
    pallas_call x1, Pallas kernels, shards(): pl.pallas_call(functools.partial(kernel, total_count), name='sinkhorn', o...  177 us

profile of v6, /device:TPU:1, one launch (start us, length us, event | category | flops | bytes accessed | tf_op | source)
XLA Modules:
  0.0 179.1 jit_solution(7919706259196937323)
XLA Ops:
  0.6 176.6 %sinkhorn.1 = (f32[2,32,2048]{2,1,0:T(8,128)}, f32[2,32,128]{2,1,0:T(8,128)}, f32[1,128]{1,0:T(1,128)}) custom-call(f32[64,2048]{1,0:T(8,128)} %x_ref.1, f32[64,2048]{1,0:T(8,128)} %y_ref.1, f32[16,128]{1,0:T(8,128)} %bitcast.4, f32[16,128]{1,0:T(8,128)} %bitcast.5, f32[32,2048]{1,0:T(8,128)} %left_ref.1, f32[32,2048]{1,0:T(8,128)} %right_ref.1, f32[1,32]{1,0:T(1,128)} %bitcast.6), custom_call_target="tpu_custom_call" | custom-call | tf_op jit(solution)/shard_map/sinkhorn/pallas_call | solution.py:528
  177.3 1.9 %finish.1 = (f32[32,2048]{1,0:T(8,128)}, f32[32,2048]{1,0:T(8,128)}, f32[1,32]{1,0:T(1,128)}) custom-call(f32[2,32,2048]{2,1,0:T(8,128)} %get-tuple-element.9.ku_ref, f32[2,32,128]{2,1,0:T(8,128)} %get-tuple-element.10.vo_ref, f32[1,128]{1,0:T(1,128)} %get-tuple-element.11.w_ref), custom_call_target="tpu_custom_call" | custom-call | tf_op jit(solution)/shard_map/finish/pallas_call | solution.py:584
